TPU v7x, 8 devices: a whole 2x2x1 slice. The times are simulated.
8 devices in a mesh: col: 2 (over z, y), row: 4 (over x, core).
Axes of the slice: x: 2, y: 2, z: 1, core: 2. Of those that a mesh axis runs over, the one named last changes fastest.
Arguments:
- inter_mask: int32 [4096, 65536], P('row', 'col')
- emb_user: bfloat16 [4096, 64], P(('row', 'col'))
- emb_item: bfloat16 [65536, 64], P(('col', 'row'))
- triples: int32 [4096, 3], replicated
Outputs:
- output 1: bfloat16 [4096, 64], P(('row', 'col'))
- output 2: bfloat16 [65536, 64], P(('col', 'row'))
- output 3: float32 [4096], replicated
All inputs are finite; a program needn't handle non-finite values.
Results may differ from a plain program's by a relative error of at most 0.00805716.
Values are sent between devices in bfloat16 or wider.
A program may use at most 1 GiB of HBM per device.

v0:
```python
import jax
import jax.numpy as jnp
from jax import lax
from jax.sharding import PartitionSpec as P

LAYERS = 3


def solution(mesh):
    row_count = mesh.shape["row"]
    col_count = mesh.shape["col"]

    def lookup(emb_table, row_ids, row_start):
        local_ids = row_ids - row_start
        is_owned = (local_ids >= 0) & (local_ids < emb_table.shape[0])
        rows_got = jnp.take(emb_table, jnp.clip(local_ids, 0, emb_table.shape[0] - 1), axis=0).astype(jnp.float32)
        return jnp.where(is_owned[:, None], rows_got, 0.0)

    def device_body(mask_blk, user_shard, item_shard, triples):
        row_idx = lax.axis_index("row")
        col_idx = lax.axis_index("col")
        deg_user = lax.psum(jnp.sum(mask_blk, axis=1), "col")
        deg_item = lax.psum(jnp.sum(mask_blk, axis=0), "row")
        scale_user = lax.rsqrt(jnp.maximum(deg_user, 1).astype(jnp.float32))
        scale_item = lax.rsqrt(jnp.maximum(deg_item, 1).astype(jnp.float32))
        adj_norm = (mask_blk.astype(jnp.float32) * scale_user[:, None] * scale_item[None, :]).astype(jnp.bfloat16)
        cur_user = user_shard
        cur_item = item_shard
        total_user = user_shard.astype(jnp.float32)
        total_item = item_shard.astype(jnp.float32)
        for layer_idx in range(LAYERS):
            item_panel = lax.all_gather(cur_item, "row", axis=0, tiled=True)
            user_panel = lax.all_gather(cur_user, "col", axis=0, tiled=True)
            user_part = jnp.dot(adj_norm, item_panel, preferred_element_type=jnp.float32)
            item_part = jnp.einsum("ui,ud->id", adj_norm, user_panel, preferred_element_type=jnp.float32)
            cur_user = lax.psum_scatter(user_part, "col", scatter_dimension=0, tiled=True).astype(jnp.bfloat16)
            cur_item = lax.psum_scatter(item_part, "row", scatter_dimension=0, tiled=True).astype(jnp.bfloat16)
            total_user = total_user + cur_user.astype(jnp.float32)
            total_item = total_item + cur_item.astype(jnp.float32)
        out_user = (total_user / (LAYERS + 1)).astype(jnp.bfloat16)
        out_item = (total_item / (LAYERS + 1)).astype(jnp.bfloat16)
        user_start = (row_idx * col_count + col_idx) * out_user.shape[0]
        item_start = (col_idx * row_count + row_idx) * out_item.shape[0]
        picked = jnp.concatenate([
            lookup(out_user, triples[:, 0], user_start),
            lookup(out_item, triples[:, 1], item_start),
            lookup(out_item, triples[:, 2], item_start),
        ], axis=0)
        picked = lax.psum(picked, ("row", "col"))
        batch_n = triples.shape[0]
        vec_user = picked[:batch_n]
        vec_pos = picked[batch_n:2 * batch_n]
        vec_neg = picked[2 * batch_n:]
        margin = jnp.sum(vec_user * vec_pos, axis=1) - jnp.sum(vec_user * vec_neg, axis=1)
        bpr_loss = jax.nn.softplus(-margin)
        return out_user, out_item, bpr_loss

    return jax.shard_map(
        device_body,
        mesh=mesh,
        in_specs=(P("row", "col"), P(("row", "col"), None), P(("col", "row"), None), P()),
        out_specs=(P(("row", "col"), None), P(("col", "row"), None), P()),
        check_vma=False,
    )
```

profile of v0, /device:TPU:0, one launch (start us, length us, event | category | flops | bytes accessed | tf_op | source)
XLA Modules:
  0.0 669.3 jit_solution(14267362524772105214)
XLA Ops:
  7.2 40.8 %fusion.4 = (s32[1024]{0:T(1024)S(1)}, s32[32768]{0:T(1024)}) fusion(s32[1024,32768]{1,0:T(8,128)} %param.6), kind=kLoop, calls=%fused_computation.34 | loop fusion | flops 67075072 | bytes 134352896 | tf_op jit(solution)/shard_map/reduce_sum | solution.py:22
  48.8 5.6 psum.21
  54.5 4.9 all_gather.19
  59.4 17.7 %all-reduce.3.cloned.1.call-done = s32[32768]{0:T(1024)} async-done(((s32[32768]{0:T(1024)}), s32[32768]{0:T(1024)}) %all-reduce.3.cloned.1.call-update) | async-done | bytes 131088 | tf_op jit(solution)/shard_map/psum | solution.py:23
  77.2 0.9 convert_rsqrt_fusion
  78.1 64.1 %multiply_convert_fusion = bf16[1024,32768]{1,0:T(8,128)(2,1)} fusion(s32[1024,32768]{1,0:T(8,128)} %param.6, f32[32768]{0:T(1024)S(1)} %convert_rsqrt_fusion, f32[1024]{0:T(1024)S(1)} %convert_rsqrt_fusion.1), kind=kLoop, calls=%fused_computation.3 | loop fusion | flops 134217728 | bytes 201461760 | tf_op jit(solution)/shard_map/convert_element_type | solution.py:26
  142.2 26.6 %fusion.8 = f32[32768,64]{0,1:T(8,128)} fusion(bf16[1024,64]{0,1:T(8,128)(2,1)S(1)} %all_gather.19, bf16[1024,32768]{1,0:T(8,128)(2,1)} %multiply_convert_fusion), kind=kOutput, calls=%fused_computation.38 | convolution fusion | flops 4294967296 | bytes 75628544 | tf_op jit(solution)/shard_map/ui,ud->id/dot_general | solution.py:35
  169.0 29.9 %fusion.5 = f32[1024,64]{0,1:T(8,128)} fusion(bf16[1024,32768]{1,0:T(8,128)(2,1)} %multiply_convert_fusion, bf16[32768,64]{0,1:T(8,128)(2,1)} %all-gather.4.cloned.1.call-done), kind=kOutput, calls=%fused_computation.35 | convolution fusion | flops 4294967296 | bytes 71565312 | tf_op jit(solution)/shard_map/dot_general | solution.py:34
  198.9 35.2 %reduce-scatter.9.cloned.1.call-done = f32[8192,64]{0,1:T(8,128)} async-done(((f32[32768,64]{0,1:T(8,128)}), f32[8192,64]{0,1:T(8,128)}) %reduce-scatter.9.cloned.1.call-update) | async-done | bytes 2097168 | tf_op jit(solution)/shard_map/reduce_scatter | solution.py:37
  234.2 2.7 convert_element_type.76
  236.9 8.2 %reduce-scatter.7.cloned.1.call-done = f32[512,64]{0,1:T(8,128)} async-done(((f32[1024,64]{0,1:T(8,128)}), f32[512,64]{0,1:T(8,128)}) %reduce-scatter.7.cloned.1.call-update) | async-done | bytes 131088 | tf_op jit(solution)/shard_map/reduce_scatter | solution.py:36
  246.0 4.9 all_gather.21
  251.0 27.6 %all-gather.6.cloned.1.call-done = bf16[32768,64]{0,1:T(8,128)(2,1)} async-done(((bf16[8192,64]{0,1:T(8,128)(2,1)}), bf16[32768,64]{0,1:T(8,128)(2,1)}) %all-gather.6.cloned.1.call-update) | async-done | bytes 4194320 | tf_op jit(solution)/shard_map/all_gather | solution.py:32
  278.6 29.8 %fusion.6 = f32[1024,64]{0,1:T(8,128)} fusion(bf16[1024,32768]{1,0:T(8,128)(2,1)} %multiply_convert_fusion, bf16[32768,64]{0,1:T(8,128)(2,1)} %all-gather.6.cloned.1.call-done), kind=kOutput, calls=%fused_computation.36 | convolution fusion | flops 4294967296 | bytes 71565312 | tf_op jit(solution)/shard_map/dot_general | solution.py:34
  308.7 26.6 %fusion.9 = f32[32768,64]{0,1:T(8,128)} fusion(bf16[1024,64]{0,1:T(8,128)(2,1)S(1)} %all_gather.21, bf16[1024,32768]{1,0:T(8,128)(2,1)} %multiply_convert_fusion), kind=kOutput, calls=%fused_computation.39 | convolution fusion | flops 4294967296 | bytes 75628544 | tf_op jit(solution)/shard_map/ui,ud->id/dot_general | solution.py:35
  336.4 4.9 all_gather.23
  341.3 26.7 %fusion.10 = f32[32768,64]{0,1:T(8,128)} fusion(bf16[1024,64]{0,1:T(8,128)(2,1)S(1)} %all_gather.23, bf16[1024,32768]{1,0:T(8,128)(2,1)} %multiply_convert_fusion), kind=kOutput, calls=%fused_computation.40 | convolution fusion | flops 4294967296 | bytes 75628544 | tf_op jit(solution)/shard_map/ui,ud->id/dot_general | solution.py:35
  368.1 32.5 %reduce-scatter.13.cloned.1.call-done = f32[8192,64]{0,1:T(8,128)} async-done(((f32[32768,64]{0,1:T(8,128)}), f32[8192,64]{0,1:T(8,128)}) %reduce-scatter.13.cloned.1.call-update) | async-done | bytes 2097168 | tf_op jit(solution)/shard_map/reduce_scatter | solution.py:37
  400.6 67.7 %reduce-scatter.17.cloned.1.call-done = f32[8192,64]{0,1:T(8,128)} async-done(((f32[32768,64]{0,1:T(8,128)}), f32[8192,64]{0,1:T(8,128)}) %reduce-scatter.17.cloned.1.call-update) | async-done | bytes 2097168 | tf_op jit(solution)/shard_map/reduce_scatter | solution.py:37
  468.3 4.0 multiply_convert_fusion.1
  473.4 1.1 copy.8
  474.5 15.0 %gather_fusion.1 = bf16[4096,64]{1,0:T(8,128)(2,1)} fusion(bf16[8192,64]{1,0:T(8,128)(2,1)S(1)} %copy.8, s32[4096]{0:T(1024)S(1)} %fusion.2), kind=kCustom, calls=%fused_computation.clone | custom fusion | bytes 1064960 | tf_op jit(solution)/shard_map/jit(_take)/gather | solution.py:16
  489.5 15.0 %gather_fusion.2 = bf16[4096,64]{1,0:T(8,128)(2,1)} fusion(bf16[8192,64]{1,0:T(8,128)(2,1)S(1)} %copy.8, s32[4096]{0:T(1024)S(1)} %fusion.3), kind=kCustom, calls=%fused_computation.1.clone | custom fusion | bytes 1064960 | tf_op jit(solution)/shard_map/jit(_take)/gather | solution.py:16
  504.5 29.9 %fusion.7 = f32[1024,64]{0,1:T(8,128)} fusion(bf16[1024,32768]{1,0:T(8,128)(2,1)} %multiply_convert_fusion, bf16[32768,64]{0,1:T(8,128)(2,1)} %all-gather.8.cloned.1.call-done), kind=kOutput, calls=%fused_computation.37 | convolution fusion | flops 4294967296 | bytes 71565312 | tf_op jit(solution)/shard_map/dot_general | solution.py:34
  534.7 7.0 %convert_select_fusion = (f32[4096,64]{1,0:T(8,128)S(1)}, f32[4096,64]{1,0:T(8,128)}) fusion(bf16[4096,64]{1,0:T(8,128)(2,1)} %gather_fusion.2, pred[4096]{0:T(1024)(128)(4,1)S(1)} %compare_and_fusion, pred[4096]{0:T(1024)(128)(4,1)S(1)} %get-tuple-element.16, bf16[4096,64]{1,0:T(8,128)(2,1)S(1)} %copy-done.3, pred[4096]{0:T(1024)(128)(4,1)S(1)} %compare_and_fusion.1, ...), kind=kLoop, calls=%fused_computation.9 | loop fusion | flops 1572864 | bytes 3162112 | tf_op jit(solution)/shard_map/jit(_where)/select_n | solution.py:17
  541.7 1.8 reduce-scatter.15.cloned.1.call-done
  543.5 0.9 multiply_convert_fusion.2
  544.6 12.1 %gather_fusion = bf16[4096,64]{1,0:T(8,128)(2,1)S(1)} fusion(bf16[512,64]{1,0:T(8,128)(2,1)S(1)} %copy.7, s32[4096]{0:T(1024)S(1)} %broadcast_clamp_fusion), kind=kCustom, calls=%fused_computation.2 | custom fusion | bytes 1064960 | tf_op jit(solution)/shard_map/jit(_take)/gather | solution.py:16
  556.8 1.3 convert_select_fusion.2
  558.3 7.2 %pad_maximum_fusion = f32[12288,64]{1,0:T(8,128)} fusion(f32[4096,64]{1,0:T(8,128)S(1)} %get-tuple-element.20, f32[4096,64]{1,0:T(8,128)S(1)} %copy-done, f32[4096,64]{1,0:T(8,128)S(1)} %convert_select_fusion.2), kind=kLoop, calls=%fused_computation.4 | loop fusion | flops 1572864 | bytes 6291456 | tf_op jit(solution)/shard_map/concatenate | solution.py:44
  565.6 92.5 %all-reduce.5.cloned.1.call-done = f32[12288,64]{1,0:T(8,128)} async-done(((f32[12288,64]{1,0:T(8,128)}), f32[12288,64]{1,0:T(8,128)}) %all-reduce.5.cloned.1.call-update) | async-done | bytes 3145744 | tf_op jit(solution)/shard_map/psum | solution.py:49
  658.1 4.0 fusion
  (61 shorter events, 5.7 us)
Async XLA Ops:
  7.2 47.3 %copy-start.6 = (bf16[512,64]{0,1:T(8,128)(2,1)S(1)}, bf16[512,64]{0,1:T(8,128)(2,1)}, u32[]{:S(2)}) copy-start(bf16[512,64]{0,1:T(8,128)(2,1)} %param.7) | copy-start | bytes 196612
  7.2 70.0 %all-reduce.3.cloned.1.call-start = ((), (), s32[]{:S(2)}) async-start(), calls=%async_computation.6 | async-start | bytes 262144 | tf_op jit(solution)/shard_map/psum | solution.py:23
  48.0 121.0 %all-gather.4.cloned.1.call-start = ((), (), s32[]{:S(2)}) async-start(), calls=%async_computation.7 | async-start | bytes 5242880 | tf_op jit(solution)/shard_map/all_gather | solution.py:32
  48.8 185.4 %reduce-scatter.9.cloned.1.call-start = ((), (), s32[]{:S(2)}) async-start(), calls=%async_computation.9 | async-start | bytes 10485760 | tf_op jit(solution)/shard_map/reduce_scatter | solution.py:37
  168.9 76.2 %reduce-scatter.7.cloned.1.call-start = ((), (), s32[]{:S(2)}) async-start(), calls=%async_computation.8 | async-start | bytes 393216 | tf_op jit(solution)/shard_map/reduce_scatter | solution.py:36
  198.9 79.7 %all-gather.6.cloned.1.call-start = ((), (), s32[]{:S(2)}) async-start(), calls=%async_computation.10 | async-start | bytes 5242880 | tf_op jit(solution)/shard_map/all_gather | solution.py:32
  236.9 98.6 %reduce-scatter.11.cloned.1.call-start = ((), (), s32[]{:S(2)}) async-start(), calls=%async_computation.11 | async-start | bytes 393216 | tf_op jit(solution)/shard_map/reduce_scatter | solution.py:36
  308.5 92.2 %reduce-scatter.13.cloned.1.call-start = ((), (), s32[]{:S(2)}) async-start(), calls=%async_computation.12 | async-start | bytes 10485760 | tf_op jit(solution)/shard_map/reduce_scatter | solution.py:37
  335.4 132.9 %reduce-scatter.17.cloned.1.call-start = ((), (), s32[]{:S(2)}) async-start(), calls=%async_computation.15 | async-start | bytes 10485760 | tf_op jit(solution)/shard_map/reduce_scatter | solution.py:37
  368.0 100.3 %copy-start.1 = (f32[8192,64]{0,1:T(8,128)S(1)}, f32[8192,64]{0,1:T(8,128)}, u32[]{:S(2)}) copy-start(f32[8192,64]{0,1:T(8,128)} %reduce-scatter.9.cloned.1.call-done) | copy-start | bytes 6291460
  368.1 104.3 %copy-start.9 = (s32[4096,3]{0,1:T(4,128)S(1)}, s32[4096,3]{0,1:T(4,128)}, u32[]{:S(2)}) copy-start(s32[4096,3]{0,1:T(4,128)} %param.9) | copy-start | bytes 147460
  368.1 136.4 %all-gather.8.cloned.1.call-start = ((), (), s32[]{:S(2)}) async-start(), calls=%async_computation.13 | async-start | bytes 5242880 | tf_op jit(solution)/shard_map/all_gather | solution.py:32
  472.3 17.2 %copy-start.2 = (bf16[8192,64]{0,1:T(8,128)(2,1)}, bf16[8192,64]{0,1:T(8,128)(2,1)S(1)}, u32[]{:S(2)}) copy-start(bf16[8192,64]{0,1:T(8,128)(2,1)S(1)} %get-tuple-element.13) | copy-start | bytes 3145732
  472.3 71.2 %reduce-scatter.15.cloned.1.call-start = ((), (), s32[]{:S(2)}) async-start(), calls=%async_computation.14 | async-start | bytes 393216 | tf_op jit(solution)/shard_map/reduce_scatter | solution.py:36
  504.5 30.2 %copy-start.3 = (bf16[4096,64]{1,0:T(8,128)(2,1)S(1)}, bf16[4096,64]{1,0:T(8,128)(2,1)}, u32[]{:S(2)}) copy-start(bf16[4096,64]{1,0:T(8,128)(2,1)} %gather_fusion.1) | copy-start | bytes 1572868
  534.4 9.1 %copy-start.4 = (f32[512,64]{0,1:T(8,128)S(1)}, f32[512,64]{0,1:T(8,128)}, u32[]{:S(2)}) copy-start(f32[512,64]{0,1:T(8,128)} %reduce-scatter.7.cloned.1.call-done) | copy-start | bytes 393220
  534.4 9.1 %copy-start.5 = (f32[512,64]{0,1:T(8,128)S(1)}, f32[512,64]{0,1:T(8,128)}, u32[]{:S(2)}) copy-start(f32[512,64]{0,1:T(8,128)} %reduce-scatter.11.cloned.1.call-done) | copy-start | bytes 393220
  534.4 9.1 %copy-start.7 = (bf16[512,64]{0,1:T(8,128)(2,1)S(1)}, bf16[512,64]{0,1:T(8,128)(2,1)}, u32[]{:S(2)}) copy-start(bf16[512,64]{0,1:T(8,128)(2,1)} %param.7) | copy-start | bytes 196612
  534.4 123.6 %all-reduce.5.cloned.1.call-start = ((), (), s32[]{:S(2)}) async-start(), calls=%async_computation.16 | async-start | bytes 12582912 | tf_op jit(solution)/shard_map/psum | solution.py:49
  544.4 12.3 %copy-start.8 = (bf16[512,64]{0,1:T(8,128)(2,1)}, bf16[512,64]{0,1:T(8,128)(2,1)S(1)}, u32[]{:S(2)}) copy-start(bf16[512,64]{0,1:T(8,128)(2,1)S(1)} %multiply_convert_fusion.2) | copy-start | bytes 196612
  544.6 12.2 %copy-start.10 = (pred[4096]{0:T(1024)(128)(4,1)S(1)}, pred[4096]{0:T(1024)(128)(4,1)}, u32[]{:S(2)}) copy-start(pred[4096]{0:T(1024)(128)(4,1)} %get-tuple-element.11) | copy-start | bytes 12292
  544.6 12.2 %copy-start.11 = (pred[4096]{0:T(1024)(128)(4,1)S(1)}, pred[4096]{0:T(1024)(128)(4,1)}, u32[]{:S(2)}) copy-start(pred[4096]{0:T(1024)(128)(4,1)} %get-tuple-element.17) | copy-start | bytes 12292
  556.7 1.6 copy-start
Sparse Core Ops, SparseCore 0:
  48.1 28.9 all-reduce.2
  78.7 31.4 all-gather.3
  169.0 65.0 reduce-scatter.8
  236.2 8.8 reduce-scatter.6
  247.1 31.4 all-gather.5
  308.6 8.8 reduce-scatter.10
  335.5 65.0 reduce-scatter.12
  403.2 65.0 reduce-scatter.16
  472.4 31.4 all-gather.7
  534.6 8.8 reduce-scatter.14
  565.7 92.3 all-reduce.4
where the time goes:
time: 670 us; the launch traced here: 669 us
  waiting for transfers between devices  284 us (42%)
  matrix products  170 us (25%)
  other arithmetic  136 us (20%)
  local copies, waits for them, and re-layouts  43.7 us (7%)
  blocking collectives  20.5 us (3%)
  between operations  14.1 us (2%)
    reduce_scatter x3, waiting for transfers between devices, device_body(): lax.psum_scatter(item_part, 'row', scatter_dimension=0, tiled=True)  135 us
    psum x1, waiting for transfers between devices, device_body(): picked = lax.psum(picked, ('row', 'col'))  92.5 us
    dot_general x3, matrix products, device_body(): jnp.dot(adj_norm, item_panel, preferred_element_type=jnp.float32)  89.6 us
    dot_general x3, matrix products, device_body(): jnp.einsum('ui,ud->id', adj_norm, user_panel, preferred_element_type=jnp....  80 us
    convert_element_type x1, other arithmetic, device_body(): (mask_blk.astype(jnp.float32) * scale_user[:, None] * scale_item[None, :]...  64.1 us
    gather x3, local copies, waits for them, and re-layouts, lookup(): jnp.take(emb_table, jnp.clip(local_ids, 0, emb_table.shape[0] - 1), axis=0)  42.2 us
    reduce_sum x1, other arithmetic, device_body(): deg_user = lax.psum(jnp.sum(mask_blk, axis=1), 'col')  40.8 us
    all_gather x3, waiting for transfers between devices, device_body(): item_panel = lax.all_gather(cur_item, 'row', axis=0, tiled=True)  27.7 us
  transfers between devices with their start and end apart: 11, of which 8 were waited for; matrix products, arithmetic and copies ran while one was open for 33% of the time, Pallas kernels for 0%

commit v1 on v0

v1 whole, which is shorter than its diff:
```python
import jax
import jax.numpy as jnp
from jax import lax
from jax.experimental import pallas as pl
from jax.experimental.pallas import tpu as pltpu
from jax.sharding import PartitionSpec as P

LAYERS = 3
F8 = jnp.float8_e4m3fn
BF = jnp.bfloat16
F32 = jnp.float32
MESH = pl.DeviceIdType.MESH

EMB = 64
USERS = 1024
HALF = 512
QUART = 8192
CH = 1024
NCH = 8
NBLK = 32
PIECE = 256
RING = 7
UP_U, DN_U = 256.0, 1.0 / 256.0
UP_I, DN_I = 64.0, 1.0 / 64.0
LAG_B, LAG_C, LAG_D = 2, 3, 4


def _scale(val, s8):
    rows, cols = val.shape
    return (val.reshape(rows // 8, 8, cols) * s8[None]).reshape(rows, cols)


def _main_kernel(mask, eu0, ei0, out_i, ua,
                 m8, stage, pan, snd_a, rcv_a, snd_b, rcv_b, xs, xr,
                 uacc, yr, raw, eus, cs, csr, sib, cacc, rs, rsum, rsum_r, su,
                 st_sem, ld_sem, agx_s, agx_r, agd_s, agd_r, agf_s, agf_r, cs_s, cs_r,
                 rs_s, rs_r, a_s, a_r, b_s, b_r, x_s, x_r, y_s, y_r, w_s, w_r, g_s, g_r):
    c = lax.axis_index("col")
    r = lax.axis_index("row")
    x = r // 2
    k = r % 2
    r_par = 2 * x + (1 - k)
    r_xp = 2 * (1 - x) + k
    r_xq = 2 * (1 - x) + (1 - k)
    par = (c, r_par)
    xpe = (c, r_xp)
    xpa = (c, r_xq)
    ype = (1 - c, r)

    def rcopy(src, dst, ss, rsm, dev):
        return pltpu.make_async_remote_copy(src_ref=src, dst_ref=dst, send_sem=ss, recv_sem=rsm,
                                            device_id=dev, device_id_type=MESH)

    def piece(p):
        blk = p // 4
        row = pl.multiple_of((p % 4) * PIECE, PIECE)
        col = pl.multiple_of((blk % 4) * QUART + (blk // 4) * CH, CH)
        return pltpu.make_async_copy(mask.at[pl.ds(row, PIECE), pl.ds(col, CH)],
                                     stage.at[p % RING], st_sem.at[p % RING])

    for p in range(RING):
        piece(p).start()

    def own_load(j):
        return pltpu.make_async_copy(ei0.at[:, pl.ds(pl.multiple_of(j * CH, CH), CH)],
                                     pan.at[0, j * 4 + r], ld_sem.at[j])

    user_load = pltpu.make_async_copy(eu0, raw.at[0, c], ld_sem.at[NCH])
    for j in range(NCH):
        own_load(j).start()
    user_load.start()

    barrier = pltpu.get_barrier_semaphore()
    for cc in range(2):
        for rr in range(4):
            pl.semaphore_signal(barrier, inc=1, device_id=(cc, rr), device_id_type=MESH)
    pl.semaphore_wait(barrier, 8)

    def ag_x(a, j, q):
        i = a * NCH + j
        ref = pan.at[a, j * 4 + q]
        return rcopy(ref, ref, agx_s.at[i], agx_r.at[i], xpe)

    def ag_d(a, j, q):
        i = a * NCH + j
        ref = pan.at[a, j * 4 + q]
        return rcopy(ref, ref, agd_s.at[i], agd_r.at[i], par)

    def ag_f(a, j, q):
        i = a * NCH + j
        ref = pan.at[a, j * 4 + q]
        return rcopy(ref, ref, agf_s.at[i], agf_r.at[i], par)

    for j in range(NCH):
        own_load(j).wait()
        ag_x(0, j, r).start()
        ag_d(0, j, r).start()
    user_load.wait()
    w0 = rcopy(raw.at[0, c], raw.at[0, c], w_s.at[0], w_r.at[0], ype)
    w0.start()

    rs[...] = jnp.zeros_like(rs)
    uacc[...] = jnp.zeros_like(uacc)

    def cs_copy(rel, g, dev):
        return rcopy(cs.at[pl.ds(g * 4, 4)], csr.at[rel, pl.ds(g * 4, 4)], cs_s.at[rel, g], cs_r.at[rel, g], dev)

    def user_prod(a, b):
        es = _scale(pan[a, b].astype(F32), sib[b] * DN_U).astype(BF)
        got = lax.dot_general(es, m8[b], (((1,), (1,)), ((), ())), preferred_element_type=F32)
        uacc[0] += got[:, :HALF]
        uacc[1] += got[:, HALF:]

    def first_users(g):
        for rel, dev in ((0, par), (1, xpe), (2, xpa)):
            cs_copy(rel, g, dev).wait_recv()
        ag_d(0, g, r_par).wait_recv()
        ag_f(0, g, r_xq).wait_recv()

        @pl.loop(0, 4)
        def _(q):
            b = g * 4 + q
            deg = cs[b] + csr[0, b] + csr[1, b] + csr[2, b]
            sib[b] = jnp.broadcast_to(lax.rsqrt(jnp.maximum(deg, 1.0)), (8, CH))
            user_prod(0, b)

    @pl.loop(0, NCH)
    def _(g):
        @pl.loop(0, 4)
        def _(q):
            b = g * 4 + q
            cacc[...] = jnp.zeros_like(cacc)

            @pl.loop(0, 4)
            def _(s):
                p = b * 4 + s
                piece(p).wait()
                slot = p % RING

                @pl.loop(0, PIECE // 32)
                def _(i):
                    rows = pl.ds(pl.multiple_of(i * 32, 32), 32)
                    dst = pl.ds(pl.multiple_of(s * PIECE + i * 32, 32), 32)
                    f = stage[slot, rows, :].astype(F32)
                    m8[b, dst, :] = f.astype(F8)
                    cacc[...] += jnp.sum(f.reshape(4, 8, CH), axis=0)
                    part = f[:, :128]
                    for w in range(1, CH // 128):
                        part = part + f[:, w * 128:(w + 1) * 128]
                    rs[dst, :] += part

                @pl.when(p + RING < 4 * NBLK)
                def _():
                    piece(p + RING).start()

            cs[b] = jnp.sum(cacc[...], axis=0, keepdims=True)

        for rel, dev in ((0, par), (1, xpe), (2, xpa)):
            cs_copy(rel, g, dev).start()
        ag_x(0, g, r_xp).wait_recv()
        ag_f(0, g, r_xp).start()

        @pl.when(g >= 1)
        def _():
            first_users(g - 1)

    rsum[...] = lax.dot_general(jnp.ones((8, 128), BF), rs[...].astype(BF), (((1,), (1,)), ((), ())),
                                preferred_element_type=F32)
    rs_copy = rcopy(rsum, rsum_r, rs_s.at[0], rs_r.at[0], ype)
    rs_copy.start()
    first_users(NCH - 1)
    rs_copy.wait()
    w0.wait()
    deg_u = lax.rsqrt(jnp.maximum(rsum[...] + rsum_r[...], 1.0))
    su[0] = deg_u[:, :HALF]
    su[1] = deg_u[:, HALF:]

    def user_operand(lay):
        for h in range(2):
            eus[lay, :, h * HALF:(h + 1) * HALF] = _scale(raw[lay, h].astype(F32), su[h] * DN_I).astype(BF)

    user_operand(0)

    def prod(lay, b):
        return jnp.dot(eus[lay], m8[b], preferred_element_type=F32)

    def cp_a(g):
        return rcopy(snd_a.at[g % 2], rcv_a.at[g % 2], a_s.at[g % 2], a_r.at[g % 2], par)

    def cp_b(g):
        return rcopy(snd_b.at[g % 4], rcv_b.at[g % 4], b_s.at[g % 4], b_r.at[g % 4], par)

    def cp_x(g):
        return rcopy(xs.at[g % 4], xr.at[g % 8], x_s.at[g % 4], x_r.at[g % 8], xpe)

    def step_a(g):
        lay = g // NCH
        b = (g % NCH) * 4

        @pl.when(g >= 2)
        def _():
            cp_a(g - 2).wait_send()

        snd_a[g % 2] = prod(lay, b + r_xq)
        cp_a(g).start()

        @pl.when(g >= 4)
        def _():
            cp_x(g - 4).wait_send()

        xs[g % 4] = prod(lay, b + r_xp)
        cp_a(g).wait_recv()
        xs[g % 4] += rcv_a[g % 2]
        cp_x(g).start()

        @pl.when(g >= 4)
        def _():
            cp_b(g - 4).wait_send()

        snd_b[g % 4] = prod(lay, b + r_par)
        cp_b(g).start()

    def step_b(g):
        lay = g // NCH
        j = g % NCH
        b = j * 4 + r
        own = prod(lay, b)
        cp_b(g).wait_recv()
        own = own + rcv_b[g % 4]
        cp_x(g).wait_recv()
        emb = _scale(own + xr[g % 8], sib[b] * UP_I).astype(BF)

        @pl.when(lay < 2)
        def _():
            pan[lay + 1, b] = emb
            ag_x(lay + 1, j, r).start()
            ag_d(lay + 1, j, r).start()

        @pl.when(lay == 2)
        def _():
            tot = pan[0, b].astype(F32) + pan[1, b].astype(F32) + pan[2, b].astype(F32) + emb.astype(F32)
            out_i[:, pl.ds(pl.multiple_of(j * CH, CH), CH)] = (tot * 0.25).astype(BF)

    def step_c(g):
        a = g // NCH + 1
        ag_x(a, g % NCH, r_xp).wait_recv()
        ag_f(a, g % NCH, r_xp).start()

    def step_d(g):
        a = g // NCH + 1
        j = g % NCH
        ag_d(a, j, r_par).wait_recv()
        ag_f(a, j, r_xq).wait_recv()

        @pl.loop(0, 4)
        def _(q):
            user_prod(a, j * 4 + q)

    def cp_y(lay):
        return rcopy(uacc.at[1 - c], yr.at[lay - 1], y_s.at[lay - 1], y_r.at[lay - 1], ype)

    def cp_w(lay):
        return rcopy(raw.at[lay, c], raw.at[lay, c], w_s.at[lay], w_r.at[lay], ype)

    def user_emb(lay):
        cp_y(lay).wait()
        emb = _scale(uacc[c] + yr[lay - 1], su[c] * UP_U).astype(BF)
        uacc[...] = jnp.zeros_like(uacc)
        return emb

    def finish_user(lay):
        raw[lay, c] = user_emb(lay)
        cp_w(lay).start()

    def load_user(lay):
        cp_w(lay).wait()
        user_operand(lay)

    def cp_g(i, blk, dev):
        return rcopy(ua.at[blk], ua.at[blk], g_s.at[i], g_r.at[i], dev)

    own_u = 2 * r + c
    D1, D2 = NCH - 1 + LAG_D, 2 * NCH - 1 + LAG_D

    @pl.loop(0, LAYERS * NCH + LAG_B)
    def _(t):
        @pl.when(t < LAYERS * NCH)
        def _():
            step_a(t)

        @pl.when(t == 0)
        def _():
            cp_y(1).start()

        @pl.when(t == 1)
        def _():
            finish_user(1)

        @pl.when(t == 2)
        def _():
            load_user(1)

        @pl.when(t == D1 + 1)
        def _():
            finish_user(2)

        @pl.when(t == D1 + 2)
        def _():
            load_user(2)

        @pl.when(t == D2 + 1)
        def _():
            emb = user_emb(3).astype(F32)
            tot = raw[0, c].astype(F32) + raw[1, c].astype(F32) + raw[2, c].astype(F32) + emb
            ua[own_u] = (tot * 0.25).astype(BF)
            cp_g(0, own_u, ype).start()
            cp_g(1, own_u, par).start()
            cp_g(2, own_u, xpe).start()

        @pl.when(t == D2 + 2)
        def _():
            cp_g(0, 2 * r + 1 - c, ype).wait_recv()
            cp_g(1, 2 * r_par + c, par).wait_recv()
            cp_g(2, 2 * r_xp + c, xpe).wait_recv()
            cp_g(3, 2 * r + 1 - c, par).start()
            cp_g(4, 2 * r_xp + c, par).start()
            cp_g(5, 2 * r_xp + c, ype).start()

        @pl.when(t == D2 + 3)
        def _():
            cp_g(3, 2 * r_par + 1 - c, par).wait_recv()
            cp_g(4, 2 * r_xq + c, par).wait_recv()
            cp_g(5, 2 * r_xp + 1 - c, ype).wait_recv()
            cp_g(6, 2 * r_xp + 1 - c, par).start()

        @pl.when(t == D2 + 4)
        def _():
            cp_g(6, 2 * r_xq + 1 - c, par).wait_recv()

        @pl.when(t >= LAG_B)
        def _():
            step_b(t - LAG_B)

        @pl.when((t >= LAG_C) & (t < 2 * NCH + LAG_C))
        def _():
            step_c(t - LAG_C)

        @pl.when((t >= LAG_D) & (t < 2 * NCH + LAG_D))
        def _():
            step_d(t - LAG_D)

        @pl.when(t == D1)
        def _():
            cp_y(2).start()

        @pl.when(t == D2)
        def _():
            cp_y(3).start()

    last = LAYERS * NCH
    for g in range(last - 2, last):
        cp_a(g).wait_send()
    for g in range(last - 4, last):
        cp_b(g).wait_send()
    for g in range(last - 4, last):
        cp_x(g).wait_send()
    for i in range(7):
        cp_g(i, own_u, par).wait_send()

    @pl.loop(0, NCH)
    def _(j):
        for rel, dev in ((0, par), (1, xpe), (2, xpa)):
            cs_copy(rel, j, dev).wait_send()

    @pl.loop(0, 3 * NCH)
    def _(i):
        ag_x(i // NCH, i % NCH, r).wait_send()
        ag_d(i // NCH, i % NCH, r).wait_send()
        ag_f(i // NCH, i % NCH, r_xp).wait_send()


def _main(mask, eu0, ei0):
    dma = pltpu.SemaphoreType.DMA
    any_spec = pl.BlockSpec(memory_space=pl.ANY)
    vmem = pl.BlockSpec(memory_space=pltpu.VMEM)
    return pl.pallas_call(
        _main_kernel,
        out_shape=(jax.ShapeDtypeStruct((EMB, QUART), BF), jax.ShapeDtypeStruct((8, EMB, HALF), BF)),
        in_specs=[any_spec, any_spec, any_spec],
        out_specs=(vmem, vmem),
        scratch_shapes=[
            pltpu.VMEM((NBLK, USERS, CH), F8),
            pltpu.VMEM((RING, PIECE, CH), jnp.int32),
            pltpu.VMEM((3, NBLK, EMB, CH), BF),
            pltpu.VMEM((2, EMB, CH), F32), pltpu.VMEM((2, EMB, CH), F32),
            pltpu.VMEM((4, EMB, CH), F32), pltpu.VMEM((4, EMB, CH), F32),
            pltpu.VMEM((4, EMB, CH), F32), pltpu.VMEM((8, EMB, CH), F32),
            pltpu.VMEM((2, EMB, HALF), F32), pltpu.VMEM((3, EMB, HALF), F32),
            pltpu.VMEM((3, 2, EMB, HALF), BF), pltpu.VMEM((3, EMB, USERS), BF),
            pltpu.VMEM((NBLK, 1, CH), F32), pltpu.VMEM((3, NBLK, 1, CH), F32),
            pltpu.VMEM((NBLK, 8, CH), F32), pltpu.VMEM((8, CH), F32),
            pltpu.VMEM((USERS, 128), F32), pltpu.VMEM((8, USERS), F32), pltpu.VMEM((8, USERS), F32),
            pltpu.VMEM((2, 8, HALF), F32),
            dma((RING,)), dma((NCH + 1,)),
            dma((3 * NCH,)), dma((3 * NCH,)), dma((3 * NCH,)), dma((3 * NCH,)), dma((3 * NCH,)), dma((3 * NCH,)),
            dma((3, NCH)), dma((3, NCH)), dma((1,)), dma((1,)),
            dma((2,)), dma((2,)), dma((4,)), dma((4,)), dma((4,)), dma((8,)),
            dma((3,)), dma((3,)), dma((3,)), dma((3,)), dma((7,)), dma((7,)),
        ],
        compiler_params=pltpu.CompilerParams(collective_id=0, has_side_effects=True, vmem_limit_bytes=67043328),
        name="propagate",
    )(mask, eu0, ei0)


def _lookup_kernel(uid, pid, nid, items, users, own_p, own_n, out, it, ut, pp, pn):
    for i in range(QUART // 512):
        it[i * 512:(i + 1) * 512, :EMB] = items[:, i * 512:(i + 1) * 512].astype(F32).T
    for i in range(8):
        ut[i * HALF:(i + 1) * HALF, :EMB] = users[i].astype(F32).T

    @pl.loop(0, 4096 // 16)
    def _(i):
        for w in range(16):
            t = i * 16 + w
            u = ut[pl.ds(uid[t], 1), :]
            pp[pl.ds(t, 1), :] = u * it[pl.ds(pid[t], 1), :]
            pn[pl.ds(t, 1), :] = u * it[pl.ds(nid[t], 1), :]

    @pl.loop(0, 32)
    def _(i):
        rows = pl.ds(pl.multiple_of(i * 128, 128), 128)
        sp = jnp.sum(pp[rows, :].T[:EMB], axis=0, keepdims=True)
        sn = jnp.sum(pn[rows, :].T[:EMB], axis=0, keepdims=True)
        row = pl.ds(i, 1)
        out[row, :] = (jnp.where(own_p[row, :] > 0, sp, 0.0) - jnp.where(own_n[row, :] > 0, sn, 0.0))


def _lookup(uid, pid, nid, items, users, own_p, own_n):
    vmem = pl.BlockSpec(memory_space=pltpu.VMEM)
    smem = pl.BlockSpec(memory_space=pltpu.SMEM)
    return pl.pallas_call(
        _lookup_kernel,
        out_shape=jax.ShapeDtypeStruct((32, 128), F32),
        in_specs=[smem, smem, smem, vmem, vmem, vmem, vmem],
        out_specs=vmem,
        scratch_shapes=[pltpu.VMEM((QUART, 128), F32), pltpu.VMEM((4096, 128), F32),
                        pltpu.VMEM((4096, 128), F32), pltpu.VMEM((4096, 128), F32)],
        name="lookup",
    )(uid, pid, nid, items, users, own_p, own_n)


def _loss_kernel(part, out, got, s_sem, r_sem):
    c = lax.axis_index("col")
    r = lax.axis_index("row")
    me = 2 * r + c
    barrier = pltpu.get_barrier_semaphore()
    for cc in range(2):
        for rr in range(4):
            pl.semaphore_signal(barrier, inc=1, device_id=(cc, rr), device_id_type=MESH)
    pl.semaphore_wait(barrier, 8)

    def copy(i, slot):
        dr, dc = i // 2, i % 2
        return pltpu.make_async_remote_copy(
            src_ref=part, dst_ref=got.at[slot], send_sem=s_sem.at[i], recv_sem=r_sem.at[i],
            device_id=((c + dc) % 2, (r + dr) % 4), device_id_type=MESH)

    def sender(i):
        return 2 * ((r + 4 - i // 2) % 4) + (c + i % 2) % 2

    for i in range(1, 8):
        copy(i, me).start()
    got[me] = part[...]
    for i in range(1, 8):
        copy(i, sender(i)).wait()
    m = got[0]
    for i in range(1, 8):
        m = m + got[i]
    out[...] = jnp.maximum(-m, 0.0) + jnp.log1p(jnp.exp(-jnp.abs(m)))


def _loss(part):
    vmem = pl.BlockSpec(memory_space=pltpu.VMEM)
    return pl.pallas_call(
        _loss_kernel,
        out_shape=jax.ShapeDtypeStruct((32, 128), F32),
        in_specs=[vmem],
        out_specs=vmem,
        scratch_shapes=[pltpu.VMEM((8, 32, 128), F32), pltpu.SemaphoreType.DMA((8,)), pltpu.SemaphoreType.DMA((8,))],
        compiler_params=pltpu.CompilerParams(collective_id=1, has_side_effects=True),
        name="loss",
    )(part)


def solution(mesh):
    def device_body(mask_blk, user_shard, item_shard, triples):
        row_idx = lax.axis_index("row")
        col_idx = lax.axis_index("col")
        out_it, users = _main(mask_blk, user_shard.T, item_shard.T)
        me = 2 * row_idx + col_idx
        out_ut = lax.dynamic_index_in_dim(users, me, 0, keepdims=False)
        start = (col_idx * 4 + row_idx) * QUART
        uid, pid, nid = triples[:, 0], triples[:, 1] - start, triples[:, 2] - start
        own_p = ((pid >= 0) & (pid < QUART)).astype(jnp.int32).reshape(32, 128)
        own_n = ((nid >= 0) & (nid < QUART)).astype(jnp.int32).reshape(32, 128)
        part = _lookup(uid, jnp.clip(pid, 0, QUART - 1), jnp.clip(nid, 0, QUART - 1), out_it, users, own_p, own_n)
        bpr_loss = _loss(part).reshape(4096)
        return out_ut.T, out_it.T, bpr_loss

    return jax.shard_map(
        device_body,
        mesh=mesh,
        in_specs=(P("row", "col"), P(("row", "col"), None), P(("col", "row"), None), P()),
        out_specs=(P(("row", "col"), None), P(("col", "row"), None), P()),
        check_vma=False,
    )
```

time: 670 us -> 291 us (0.43)
  waiting for transfers between devices: 284 us -> 0 us
  Pallas kernels: 0 us -> 282 us
  matrix products: 170 us -> 0 us
  other arithmetic: 136 us -> 3.22 us
  local copies, waits for them, and re-layouts: 43.7 us -> 5.06 us
  blocking collectives: 20.5 us -> 0 us
  between operations: 14.1 us -> 0.66 us
    pallas_call x0 -> x3, Pallas kernels: none -> 282 us  [the longest x1 261 us: _main(): pl.pallas_call(_main_kernel, out_shape=(jax.ShapeDtypeStruct((EMB, QUART)...]
    dot_general x6 -> x0, matrix products: 170 us -> none  [the longest x3 89.6 us: device_body(): jnp.dot(adj_norm, item_panel, preferred_element_type=jnp.float32)]
    reduce_scatter x6 -> x0, waiting for transfers between devices: 145 us -> none  [the longest x3 135 us: device_body(): lax.psum_scatter(item_part, 'row', scatter_dimension=0, tiled=True)]
    psum x2 -> x0, waiting for transfers between devices: 110 us -> none  [the longest x1 92.5 us: device_body(): picked = lax.psum(picked, ('row', 'col'))]
    convert_element_type x6 -> x1, other arithmetic: 73.6 us -> 1.59 us  [device_body(): own_n = ((nid >= 0) & (nid < QUART)).astype(jnp.int32).reshape(32, 128)]
    reduce_sum x2 -> x0, other arithmetic: 44.8 us -> none  [the longest x1 40.8 us: device_body(): deg_user = lax.psum(jnp.sum(mask_blk, axis=1), 'col')]
    gather x3 -> x0, local copies, waits for them, and re-layouts: 42.2 us -> none  [lookup(): jnp.take(emb_table, jnp.clip(local_ids, 0, emb_table.shape[0] - 1), axis=0)]
    all_gather x3 -> x0, waiting for transfers between devices: 27.7 us -> none  [device_body(): item_panel = lax.all_gather(cur_item, 'row', axis=0, tiled=True)]
  transfers between devices with their start and end apart: 11 -> 0, of which waited for: 8 -> 0; matrix products, arithmetic and copies ran while one was open for 33% -> 0% of each run, Pallas kernels for 0% -> 0%
where the time goes in v1:
time: 291 us
  Pallas kernels  282 us (97%)
  local copies, waits for them, and re-layouts  5.06 us (2%)
  other arithmetic  3.22 us (1%)
    pallas_call x1, Pallas kernels, _main(): pl.pallas_call(_main_kernel, out_shape=(jax.ShapeDtypeStruct((EMB, QUART)...  261 us
    pallas_call x1, Pallas kernels, _lookup(): pl.pallas_call(_lookup_kernel, out_shape=jax.ShapeDtypeStruct((32, 128),...  14.9 us
    pallas_call x1, Pallas kernels, _loss(): pl.pallas_call(_loss_kernel, out_shape=jax.ShapeDtypeStruct((32, 128), F3...  6.44 us

profile of v1, /device:TPU:0, one launch (start us, length us, event | category | flops | bytes accessed | tf_op | source)
XLA Modules:
  0.0 290.9 jit_solution(15009989460196158352)
XLA Ops:
  0.6 1.6 and_convert_fusion
  2.2 1.6 broadcast_clamp_fusion
  3.9 260.6 %propagate.1 = (bf16[64,8192]{1,0:T(8,128)(2,1)}, bf16[8,64,512]{2,1,0:T(8,128)(2,1)}) custom-call(s32[1024,32768]{1,0:T(8,128)} %mask.1, bf16[64,512]{1,0:T(8,128)(2,1)} %bitcast.15, bf16[64,8192]{1,0:T(8,128)(2,1)} %bitcast.14), custom_call_target="tpu_custom_call" | custom-call | tf_op jit(solution)/shard_map/propagate/pallas_call | solution.py:386
  264.5 14.9 %lookup.1.part = f32[32,128]{1,0:T(8,128)} custom-call(s32[4096]{0:T(1024)} %bitcast.19, s32[4096]{0:T(1024)} %bitcast.20, s32[4096]{0:T(1024)} %bitcast.18, bf16[64,8192]{1,0:T(8,128)(2,1)} %get-tuple-element.6.items, bf16[8,64,512]{2,1,0:T(8,128)(2,1)} %get-tuple-element.5.users, s32[32,128]{1,0:T(8,128)} %bitcast.17, s32[32,128]{1,0:T(8,128)} %bitcast.16), custom_call_target="tpu_custom_call" | custom-call | tf_op jit(solution)/shard_map/lookup/pallas_call | solution.py:441
  279.4 1.5 dynamic-slice_bitcast_fusion
  280.9 6.4 %loss.1 = f32[32,128]{1,0:T(8,128)} custom-call(f32[32,128]{1,0:T(8,128)} %lookup.1.part), custom_call_target="tpu_custom_call" | custom-call | tf_op jit(solution)/shard_map/loss/pallas_call | solution.py:484
  287.3 2.3 copy.9
  289.6 1.3 copy.10

commit v2 on v1

--- a/solution.py
+++ b/solution.py
@@ -23,6 +23,7 @@
 UP_U, DN_U = 256.0, 1.0 / 256.0
 UP_I, DN_I = 64.0, 1.0 / 64.0
 LAG_B, LAG_C, LAG_D = 2, 3, 4
+AHEAD = 2
 
 
 def _scale(val, s8):
@@ -93,7 +94,8 @@
 
     for j in range(NCH):
         own_load(j).wait()
-        ag_x(0, j, r).start()
+        if j < AHEAD:
+            ag_x(0, j, r).start()
         ag_d(0, j, r).start()
     user_load.wait()
     w0 = rcopy(raw.at[0, c], raw.at[0, c], w_s.at[0], w_r.at[0], ype)
@@ -123,6 +125,8 @@
             deg = cs[b] + csr[0, b] + csr[1, b] + csr[2, b]
             sib[b] = jnp.broadcast_to(lax.rsqrt(jnp.maximum(deg, 1.0)), (8, CH))
             user_prod(0, b)
+
+    cp_deg = rcopy(rsum, rsum_r, rs_s.at[0], rs_r.at[0], ype)
 
     @pl.loop(0, NCH)
     def _(g):
@@ -157,19 +161,25 @@
 
         for rel, dev in ((0, par), (1, xpe), (2, xpa)):
             cs_copy(rel, g, dev).start()
+
+        @pl.when(g + AHEAD < NCH)
+        def _():
+            ag_x(0, g + AHEAD, r).start()
+
+        @pl.when(g == NCH - 1)
+        def _():
+            rsum[...] = lax.dot_general(jnp.ones((8, 128), BF), rs[...].astype(BF), (((1,), (1,)), ((), ())),
+                                        preferred_element_type=F32)
+            cp_deg.start()
+
         ag_x(0, g, r_xp).wait_recv()
         ag_f(0, g, r_xp).start()
 
-        @pl.when(g >= 1)
+        @pl.when((g >= 1) & (g < NCH - 1))
         def _():
             first_users(g - 1)
 
-    rsum[...] = lax.dot_general(jnp.ones((8, 128), BF), rs[...].astype(BF), (((1,), (1,)), ((), ())),
-                                preferred_element_type=F32)
-    rs_copy = rcopy(rsum, rsum_r, rs_s.at[0], rs_r.at[0], ype)
-    rs_copy.start()
-    first_users(NCH - 1)
-    rs_copy.wait()
+    cp_deg.wait()
     w0.wait()
     deg_u = lax.rsqrt(jnp.maximum(rsum[...] + rsum_r[...], 1.0))
     su[0] = deg_u[:, :HALF]
@@ -288,15 +298,19 @@
         def _():
             step_a(t)
 
-        @pl.when(t == 0)
+        @pl.when(t < 2)
+        def _():
+            first_users(NCH - 2 + t)
+
+        @pl.when(t == 1)
         def _():
             cp_y(1).start()
 
-        @pl.when(t == 1)
+        @pl.when(t == 2)
         def _():
             finish_user(1)
 
-        @pl.when(t == 2)
+        @pl.when(t == 3)
         def _():
             load_user(1)
 
@@ -412,7 +426,11 @@
     )(mask, eu0, ei0)
 
 
-def _lookup_kernel(uid, pid, nid, items, users, own_p, own_n, out, it, ut, pp, pn):
+def _lookup_kernel(ids, tri, items, users, part, out_i, out_u, it, ut, pp, pn):
+    c = lax.axis_index("col")
+    r = lax.axis_index("row")
+    out_i[...] = items[...]
+    out_u[...] = users[2 * r + c]
     for i in range(QUART // 512):
         it[i * 512:(i + 1) * 512, :EMB] = items[:, i * 512:(i + 1) * 512].astype(F32).T
     for i in range(8):
@@ -422,31 +440,35 @@
     def _(i):
         for w in range(16):
             t = i * 16 + w
-            u = ut[pl.ds(uid[t], 1), :]
-            pp[pl.ds(t, 1), :] = u * it[pl.ds(pid[t], 1), :]
-            pn[pl.ds(t, 1), :] = u * it[pl.ds(nid[t], 1), :]
-
-    @pl.loop(0, 32)
+            u = ut[pl.ds(ids[0, t], 1), :]
+            pp[pl.ds(t, 1), :] = u * it[pl.ds(ids[1, t] & (QUART - 1), 1), :]
+            pn[pl.ds(t, 1), :] = u * it[pl.ds(ids[2, t] & (QUART - 1), 1), :]
+
+    @pl.loop(0, 8)
     def _(i):
-        rows = pl.ds(pl.multiple_of(i * 128, 128), 128)
-        sp = jnp.sum(pp[rows, :].T[:EMB], axis=0, keepdims=True)
-        sn = jnp.sum(pn[rows, :].T[:EMB], axis=0, keepdims=True)
-        row = pl.ds(i, 1)
-        out[row, :] = (jnp.where(own_p[row, :] > 0, sp, 0.0) - jnp.where(own_n[row, :] > 0, sn, 0.0))
-
-
-def _lookup(uid, pid, nid, items, users, own_p, own_n):
+        for w in range(4):
+            at = i * 4 + w
+            rows = pl.ds(pl.multiple_of(at * 128, 128), 128)
+            sp = jnp.sum(pp[rows, :].T[:EMB], axis=0, keepdims=True)
+            sn = jnp.sum(pn[rows, :].T[:EMB], axis=0, keepdims=True)
+            own_p = tri[1:2, rows] // QUART == c * 4 + r
+            own_n = tri[2:3, rows] // QUART == c * 4 + r
+            part[pl.ds(at, 1), :] = jnp.where(own_p, sp, 0.0) - jnp.where(own_n, sn, 0.0)
+
+
+def _lookup(tri, items, users):
     vmem = pl.BlockSpec(memory_space=pltpu.VMEM)
     smem = pl.BlockSpec(memory_space=pltpu.SMEM)
     return pl.pallas_call(
         _lookup_kernel,
-        out_shape=jax.ShapeDtypeStruct((32, 128), F32),
-        in_specs=[smem, smem, smem, vmem, vmem, vmem, vmem],
-        out_specs=vmem,
+        out_shape=(jax.ShapeDtypeStruct((32, 128), F32), jax.ShapeDtypeStruct((EMB, QUART), BF),
+                   jax.ShapeDtypeStruct((EMB, HALF), BF)),
+        in_specs=[smem, vmem, vmem, vmem],
+        out_specs=(vmem, vmem, vmem),
         scratch_shapes=[pltpu.VMEM((QUART, 128), F32), pltpu.VMEM((4096, 128), F32),
                         pltpu.VMEM((4096, 128), F32), pltpu.VMEM((4096, 128), F32)],
         name="lookup",
-    )(uid, pid, nid, items, users, own_p, own_n)
+    )(tri, tri, items, users)
 
 
 def _loss_kernel(part, out, got, s_sem, r_sem):
@@ -494,16 +516,8 @@
 
 def solution(mesh):
     def device_body(mask_blk, user_shard, item_shard, triples):
-        row_idx = lax.axis_index("row")
-        col_idx = lax.axis_index("col")
         out_it, users = _main(mask_blk, user_shard.T, item_shard.T)
-        me = 2 * row_idx + col_idx
-        out_ut = lax.dynamic_index_in_dim(users, me, 0, keepdims=False)
-        start = (col_idx * 4 + row_idx) * QUART
-        uid, pid, nid = triples[:, 0], triples[:, 1] - start, triples[:, 2] - start
-        own_p = ((pid >= 0) & (pid < QUART)).astype(jnp.int32).reshape(32, 128)
-        own_n = ((nid >= 0) & (nid < QUART)).astype(jnp.int32).reshape(32, 128)
-        part = _lookup(uid, jnp.clip(pid, 0, QUART - 1), jnp.clip(nid, 0, QUART - 1), out_it, users, own_p, own_n)
+        part, out_it, out_ut = _lookup(triples.T, out_it, users)
         bpr_loss = _loss(part).reshape(4096)
         return out_ut.T, out_it.T, bpr_loss
 

time: 291 us -> 278 us (0.955)
  Pallas kernels: 282 us -> 276 us
  local copies, waits for them, and re-layouts: 5.06 us -> 1.32 us
  other arithmetic: 3.22 us -> 0 us
    pallas_call x1, Pallas kernels: 261 us -> 245 us  [_main(): pl.pallas_call(_main_kernel, out_shape=(jax.ShapeDtypeStruct((EMB, QUART)...]
    pallas_call x1, Pallas kernels: 14.9 us -> 25 us  [_lookup(): pl.pallas_call(_lookup_kernel, out_shape=(jax.ShapeDtypeStruct((32, 128),...]
where the time goes in v2:
time: 278 us
  Pallas kernels  276 us (99%)
    pallas_call x1, Pallas kernels, _main(): pl.pallas_call(_main_kernel, out_shape=(jax.ShapeDtypeStruct((EMB, QUART)...  245 us
    pallas_call x1, Pallas kernels, _lookup(): pl.pallas_call(_lookup_kernel, out_shape=(jax.ShapeDtypeStruct((32, 128),...  25 us
    pallas_call x1, Pallas kernels, _loss(): pl.pallas_call(_loss_kernel, out_shape=jax.ShapeDtypeStruct((32, 128), F3...  6.44 us

profile of v2, /device:TPU:0, one launch (start us, length us, event | category | flops | bytes accessed | tf_op | source)
XLA Modules:
  0.0 278.0 jit_solution(13028703491199620243)
XLA Ops:
  0.6 244.6 %propagate.1 = (bf16[64,8192]{1,0:T(8,128)(2,1)}, bf16[8,64,512]{2,1,0:T(8,128)(2,1)}) custom-call(s32[1024,32768]{1,0:T(8,128)} %mask.1, bf16[64,512]{1,0:T(8,128)(2,1)} %bitcast.9, bf16[64,8192]{1,0:T(8,128)(2,1)} %bitcast.6), custom_call_target="tpu_custom_call" | custom-call | tf_op jit(solution)/shard_map/propagate/pallas_call | solution.py:400
  245.2 25.0 %lookup.1 = (f32[32,128]{1,0:T(8,128)}, bf16[64,8192]{1,0:T(8,128)(2,1)}, bf16[64,512]{1,0:T(8,128)(2,1)}) custom-call(s32[3,4096]{1,0:T(4,128)} %bitcast.7, s32[3,4096]{1,0:T(4,128)} %bitcast.8, bf16[64,8192]{1,0:T(8,128)(2,1)} %get-tuple-element.8.items, bf16[8,64,512]{2,1,0:T(8,128)(2,1)} %get-tuple-element.9.users), custom_call_target="tpu_custom_call" | custom-call | tf_op jit(solution)/shard_map/lookup/pallas_call | solution.py:462
  270.2 6.4 %loss.1 = f32[32,128]{1,0:T(8,128)} custom-call(f32[32,128]{1,0:T(8,128)} %get-tuple-element.12.part), custom_call_target="tpu_custom_call" | custom-call | tf_op jit(solution)/shard_map/loss/pallas_call | solution.py:506
  276.7 1.3 copy.8

commit v3 on v2

--- a/solution.py
+++ b/solution.py
@@ -23,7 +23,7 @@
 UP_U, DN_U = 256.0, 1.0 / 256.0
 UP_I, DN_I = 64.0, 1.0 / 64.0
 LAG_B, LAG_C, LAG_D = 2, 3, 4
-AHEAD = 2
+AHEAD = 3
 
 
 def _scale(val, s8):
@@ -31,7 +31,7 @@
     return (val.reshape(rows // 8, 8, cols) * s8[None]).reshape(rows, cols)
 
 
-def _main_kernel(mask, eu0, ei0, out_i, ua,
+def _main_kernel(mask, eu0, ei0, tri, out_i, ua, ids,
                  m8, stage, pan, snd_a, rcv_a, snd_b, rcv_b, xs, xr,
                  uacc, yr, raw, eus, cs, csr, sib, cacc, rs, rsum, rsum_r, su,
                  st_sem, ld_sem, agx_s, agx_r, agd_s, agd_r, agf_s, agf_r, cs_s, cs_r,
@@ -309,6 +309,9 @@
         @pl.when(t == 2)
         def _():
             finish_user(1)
+            for i in range(32):
+                for w in range(3):
+                    ids[w, i:i + 1, :] = tri[w:w + 1, i * 128:(i + 1) * 128] & ((4096 if w == 0 else QUART) - 1)
 
         @pl.when(t == 3)
         def _():
@@ -393,15 +396,16 @@
         ag_f(i // NCH, i % NCH, r_xp).wait_send()
 
 
-def _main(mask, eu0, ei0):
+def _main(mask, eu0, ei0, tri):
     dma = pltpu.SemaphoreType.DMA
     any_spec = pl.BlockSpec(memory_space=pl.ANY)
     vmem = pl.BlockSpec(memory_space=pltpu.VMEM)
     return pl.pallas_call(
         _main_kernel,
-        out_shape=(jax.ShapeDtypeStruct((EMB, QUART), BF), jax.ShapeDtypeStruct((8, EMB, HALF), BF)),
-        in_specs=[any_spec, any_spec, any_spec],
-        out_specs=(vmem, vmem),
+        out_shape=(jax.ShapeDtypeStruct((EMB, QUART), BF), jax.ShapeDtypeStruct((8, EMB, HALF), BF),
+                   jax.ShapeDtypeStruct((3, 32, 128), jnp.int32)),
+        in_specs=[any_spec, any_spec, any_spec, vmem],
+        out_specs=(vmem, vmem, vmem),
         scratch_shapes=[
             pltpu.VMEM((NBLK, USERS, CH), F8),
             pltpu.VMEM((RING, PIECE, CH), jnp.int32),
@@ -423,10 +427,10 @@
         ],
         compiler_params=pltpu.CompilerParams(collective_id=0, has_side_effects=True, vmem_limit_bytes=67043328),
         name="propagate",
-    )(mask, eu0, ei0)
-
-
-def _lookup_kernel(ids, tri, items, users, part, out_i, out_u, it, ut, pp, pn):
+    )(mask, eu0, ei0, tri)
+
+
+def _lookup_kernel(uid, pid, nid, tri, items, users, part, out_i, out_u, it, ut, pp, pn):
     c = lax.axis_index("col")
     r = lax.axis_index("row")
     out_i[...] = items[...]
@@ -436,13 +440,13 @@
     for i in range(8):
         ut[i * HALF:(i + 1) * HALF, :EMB] = users[i].astype(F32).T
 
-    @pl.loop(0, 4096 // 16)
+    @pl.loop(0, 4096 // 64)
     def _(i):
-        for w in range(16):
-            t = i * 16 + w
-            u = ut[pl.ds(ids[0, t], 1), :]
-            pp[pl.ds(t, 1), :] = u * it[pl.ds(ids[1, t] & (QUART - 1), 1), :]
-            pn[pl.ds(t, 1), :] = u * it[pl.ds(ids[2, t] & (QUART - 1), 1), :]
+        for w in range(64):
+            t = i * 64 + w
+            u = ut[pl.ds(uid[t], 1), :]
+            pp[pl.ds(t, 1), :] = u * it[pl.ds(pid[t], 1), :]
+            pn[pl.ds(t, 1), :] = u * it[pl.ds(nid[t], 1), :]
 
     @pl.loop(0, 8)
     def _(i):
@@ -456,19 +460,19 @@
             part[pl.ds(at, 1), :] = jnp.where(own_p, sp, 0.0) - jnp.where(own_n, sn, 0.0)
 
 
-def _lookup(tri, items, users):
+def _lookup(ids, tri, items, users):
     vmem = pl.BlockSpec(memory_space=pltpu.VMEM)
     smem = pl.BlockSpec(memory_space=pltpu.SMEM)
     return pl.pallas_call(
         _lookup_kernel,
         out_shape=(jax.ShapeDtypeStruct((32, 128), F32), jax.ShapeDtypeStruct((EMB, QUART), BF),
                    jax.ShapeDtypeStruct((EMB, HALF), BF)),
-        in_specs=[smem, vmem, vmem, vmem],
+        in_specs=[smem, smem, smem, vmem, vmem, vmem],
         out_specs=(vmem, vmem, vmem),
         scratch_shapes=[pltpu.VMEM((QUART, 128), F32), pltpu.VMEM((4096, 128), F32),
                         pltpu.VMEM((4096, 128), F32), pltpu.VMEM((4096, 128), F32)],
         name="lookup",
-    )(tri, tri, items, users)
+    )(ids[0].reshape(4096), ids[1].reshape(4096), ids[2].reshape(4096), tri, items, users)
 
 
 def _loss_kernel(part, out, got, s_sem, r_sem):
@@ -516,8 +520,9 @@
 
 def solution(mesh):
     def device_body(mask_blk, user_shard, item_shard, triples):
-        out_it, users = _main(mask_blk, user_shard.T, item_shard.T)
-        part, out_it, out_ut = _lookup(triples.T, out_it, users)
+        tri = triples.T
+        out_it, users, ids = _main(mask_blk, user_shard.T, item_shard.T, tri)
+        part, out_it, out_ut = _lookup(ids, tri, out_it, users)
         bpr_loss = _loss(part).reshape(4096)
         return out_ut.T, out_it.T, bpr_loss
 

time: 278 us -> 269 us (0.968)
  Pallas kernels: 276 us -> 265 us
    pallas_call x1, Pallas kernels: 25 us -> 12.8 us  [_lookup(): pl.pallas_call(_lookup_kernel, out_shape=(jax.ShapeDtypeStruct((32, 128),...]
where the time goes in v3:
time: 269 us; the launch traced here: 268 us
  Pallas kernels  265 us (99%)
  local copies, waits for them, and re-layouts  2.69 us (1%)
    pallas_call x1, Pallas kernels, _main(): pl.pallas_call(_main_kernel, out_shape=(jax.ShapeDtypeStruct((EMB, QUART)...  246 us
    pallas_call x1, Pallas kernels, _lookup(): pl.pallas_call(_lookup_kernel, out_shape=(jax.ShapeDtypeStruct((32, 128),...  12.8 us
    pallas_call x1, Pallas kernels, _loss(): pl.pallas_call(_loss_kernel, out_shape=jax.ShapeDtypeStruct((32, 128), F3...  6.44 us

profile of v3, /device:TPU:0, one launch (start us, length us, event | category | flops | bytes accessed | tf_op | source)
XLA Modules:
  0.0 268.4 jit_solution(17192416338263554364)
XLA Ops:
  0.6 245.8 %propagate.1 = (bf16[64,8192]{1,0:T(8,128)(2,1)}, bf16[8,64,512]{2,1,0:T(8,128)(2,1)}, s32[3,32,128]{2,1,0:T(8,128)}) custom-call(s32[1024,32768]{1,0:T(8,128)} %mask.1, bf16[64,512]{1,0:T(8,128)(2,1)} %bitcast.15, bf16[64,8192]{1,0:T(8,128)(2,1)} %bitcast.12, s32[3,4096]{1,0:T(4,128)} %bitcast.13), custom_call_target="tpu_custom_call" | custom-call | tf_op jit(solution)/shard_map/propagate/pallas_call | solution.py:403
  246.5 1.4 slice_bitcast_fusion
  247.8 12.8 %lookup.1 = (f32[32,128]{1,0:T(8,128)}, bf16[64,8192]{1,0:T(8,128)(2,1)}, bf16[64,512]{1,0:T(8,128)(2,1)}) custom-call(s32[4096]{0:T(1024)} %get-tuple-element.17.uid, s32[4096]{0:T(1024)} %get-tuple-element.16.pid, s32[4096]{0:T(1024)} %get-tuple-element.15.nid, s32[3,4096]{1,0:T(4,128)} %bitcast.14, bf16[64,8192]{1,0:T(8,128)(2,1)} %get-tuple-element.10.items, ...), custom_call_target="tpu_custom_call" | custom-call | tf_op jit(solution)/shard_map/lookup/pallas_call | solution.py:466
  260.6 6.4 %loss.1 = f32[32,128]{1,0:T(8,128)} custom-call(f32[32,128]{1,0:T(8,128)} %get-tuple-element.14.part), custom_call_target="tpu_custom_call" | custom-call | tf_op jit(solution)/shard_map/loss/pallas_call | solution.py:510
  267.1 1.3 copy.8

commit v4 on v3

--- a/solution.py
+++ b/solution.py
@@ -19,6 +19,7 @@
 NCH = 8
 NBLK = 32
 PIECE = 256
+STEP = 64
 RING = 7
 UP_U, DN_U = 256.0, 1.0 / 256.0
 UP_I, DN_I = 64.0, 1.0 / 64.0
@@ -59,9 +60,6 @@
         return pltpu.make_async_copy(mask.at[pl.ds(row, PIECE), pl.ds(col, CH)],
                                      stage.at[p % RING], st_sem.at[p % RING])
 
-    for p in range(RING):
-        piece(p).start()
-
     def own_load(j):
         return pltpu.make_async_copy(ei0.at[:, pl.ds(pl.multiple_of(j * CH, CH), CH)],
                                      pan.at[0, j * 4 + r], ld_sem.at[j])
@@ -70,6 +68,8 @@
     for j in range(NCH):
         own_load(j).start()
     user_load.start()
+    for p in range(RING):
+        piece(p).start()
 
     barrier = pltpu.get_barrier_semaphore()
     for cc in range(2):
@@ -141,13 +141,13 @@
                 piece(p).wait()
                 slot = p % RING
 
-                @pl.loop(0, PIECE // 32)
+                @pl.loop(0, PIECE // STEP)
                 def _(i):
-                    rows = pl.ds(pl.multiple_of(i * 32, 32), 32)
-                    dst = pl.ds(pl.multiple_of(s * PIECE + i * 32, 32), 32)
+                    rows = pl.ds(pl.multiple_of(i * STEP, STEP), STEP)
+                    dst = pl.ds(pl.multiple_of(s * PIECE + i * STEP, STEP), STEP)
                     f = stage[slot, rows, :].astype(F32)
                     m8[b, dst, :] = f.astype(F8)
-                    cacc[...] += jnp.sum(f.reshape(4, 8, CH), axis=0)
+                    cacc[...] += jnp.sum(f.reshape(STEP // 8, 8, CH), axis=0)
                     part = f[:, :128]
                     for w in range(1, CH // 128):
                         part = part + f[:, w * 128:(w + 1) * 128]
@@ -174,10 +174,6 @@
 
         ag_x(0, g, r_xp).wait_recv()
         ag_f(0, g, r_xp).start()
-
-        @pl.when((g >= 1) & (g < NCH - 1))
-        def _():
-            first_users(g - 1)
 
     cp_deg.wait()
     w0.wait()
@@ -298,22 +294,23 @@
         def _():
             step_a(t)
 
-        @pl.when(t < 2)
-        def _():
-            first_users(NCH - 2 + t)
-
-        @pl.when(t == 1)
+        @pl.when(t < 4)
+        def _():
+            first_users(2 * t)
+            first_users(2 * t + 1)
+
+        @pl.when(t == 3)
         def _():
             cp_y(1).start()
 
-        @pl.when(t == 2)
+        @pl.when(t == 4)
         def _():
             finish_user(1)
             for i in range(32):
                 for w in range(3):
                     ids[w, i:i + 1, :] = tri[w:w + 1, i * 128:(i + 1) * 128] & ((4096 if w == 0 else QUART) - 1)
 
-        @pl.when(t == 3)
+        @pl.when(t == 5)
         def _():
             load_user(1)
 

time: 269 us -> 260 us (0.967)
  Pallas kernels: 265 us -> 256 us
    pallas_call x1, Pallas kernels: 246 us -> 237 us  [_main(): pl.pallas_call(_main_kernel, out_shape=(jax.ShapeDtypeStruct((EMB, QUART)...]
where the time goes in v4:
time: 260 us
  Pallas kernels  256 us (98%)
  local copies, waits for them, and re-layouts  2.69 us (1%)
    pallas_call x1, Pallas kernels, _main(): pl.pallas_call(_main_kernel, out_shape=(jax.ShapeDtypeStruct((EMB, QUART)...  237 us
    pallas_call x1, Pallas kernels, _lookup(): pl.pallas_call(_lookup_kernel, out_shape=(jax.ShapeDtypeStruct((32, 128),...  12.8 us
    pallas_call x1, Pallas kernels, _loss(): pl.pallas_call(_loss_kernel, out_shape=jax.ShapeDtypeStruct((32, 128), F3...  6.44 us

profile of v4, /device:TPU:0, one launch (start us, length us, event | category | flops | bytes accessed | tf_op | source)
XLA Modules:
  0.0 259.8 jit_solution(7148364244308957092)
XLA Ops:
  0.6 237.2 %propagate.1 = (bf16[64,8192]{1,0:T(8,128)(2,1)}, bf16[8,64,512]{2,1,0:T(8,128)(2,1)}, s32[3,32,128]{2,1,0:T(8,128)}) custom-call(s32[1024,32768]{1,0:T(8,128)} %mask.1, bf16[64,512]{1,0:T(8,128)(2,1)} %bitcast.15, bf16[64,8192]{1,0:T(8,128)(2,1)} %bitcast.12, s32[3,4096]{1,0:T(4,128)} %bitcast.13), custom_call_target="tpu_custom_call" | custom-call | tf_op jit(solution)/shard_map/propagate/pallas_call | solution.py:400
  237.9 1.4 slice_bitcast_fusion
  239.2 12.8 %lookup.1 = (f32[32,128]{1,0:T(8,128)}, bf16[64,8192]{1,0:T(8,128)(2,1)}, bf16[64,512]{1,0:T(8,128)(2,1)}) custom-call(s32[4096]{0:T(1024)} %get-tuple-element.17.uid, s32[4096]{0:T(1024)} %get-tuple-element.16.pid, s32[4096]{0:T(1024)} %get-tuple-element.15.nid, s32[3,4096]{1,0:T(4,128)} %bitcast.14, bf16[64,8192]{1,0:T(8,128)(2,1)} %get-tuple-element.10.items, ...), custom_call_target="tpu_custom_call" | custom-call | tf_op jit(solution)/shard_map/lookup/pallas_call | solution.py:463
  252.0 6.4 %loss.1 = f32[32,128]{1,0:T(8,128)} custom-call(f32[32,128]{1,0:T(8,128)} %get-tuple-element.14.part), custom_call_target="tpu_custom_call" | custom-call | tf_op jit(solution)/shard_map/loss/pallas_call | solution.py:507
  258.5 1.3 copy.8

commit v5 on v4

--- a/solution.py
+++ b/solution.py
@@ -32,11 +32,11 @@
     return (val.reshape(rows // 8, 8, cols) * s8[None]).reshape(rows, cols)
 
 
-def _main_kernel(mask, eu0, ei0, tri, out_i, ua, ids,
+def _main_kernel(mask, eu0, ei0, tri, out_i, out_p, ua, id_u, id_p, id_n,
                  m8, stage, pan, snd_a, rcv_a, snd_b, rcv_b, xs, xr,
                  uacc, yr, raw, eus, cs, csr, sib, cacc, rs, rsum, rsum_r, su,
                  st_sem, ld_sem, agx_s, agx_r, agd_s, agd_r, agf_s, agf_r, cs_s, cs_r,
-                 rs_s, rs_r, a_s, a_r, b_s, b_r, x_s, x_r, y_s, y_r, w_s, w_r, g_s, g_r):
+                 rs_s, rs_r, a_s, a_r, b_s, b_r, x_s, x_r, y_s, y_r, w_s, w_r, g_s, g_r, o_s, o_r, l_sem, p_sem):
     c = lax.axis_index("col")
     r = lax.axis_index("row")
     x = r // 2
@@ -226,6 +226,13 @@
         snd_b[g % 4] = prod(lay, b + r_par)
         cp_b(g).start()
 
+    def cp_o(j, q):
+        ref = pan.at[1, j * 4 + q]
+        return rcopy(ref, ref, o_s.at[j], o_r.at[j], par)
+
+    def store(out, j, q, sem):
+        return pltpu.make_async_copy(pan.at[1, j * 4 + q], out.at[:, pl.ds(pl.multiple_of(j * CH, CH), CH)], sem.at[j])
+
     def step_b(g):
         lay = g // NCH
         j = g % NCH
@@ -245,7 +252,16 @@
         @pl.when(lay == 2)
         def _():
             tot = pan[0, b].astype(F32) + pan[1, b].astype(F32) + pan[2, b].astype(F32) + emb.astype(F32)
-            out_i[:, pl.ds(pl.multiple_of(j * CH, CH), CH)] = (tot * 0.25).astype(BF)
+            ag_x(1, j, r).wait_send()
+            ag_d(1, j, r).wait_send()
+            pan[1, b] = (tot * 0.25).astype(BF)
+            cp_o(j, r).start()
+            store(out_i, j, r, l_sem).start()
+
+            @pl.when(j >= 1)
+            def _():
+                cp_o(j - 1, r_par).wait_recv()
+                store(out_p, j - 1, r_par, p_sem).start()
 
     def step_c(g):
         a = g // NCH + 1
@@ -307,8 +323,8 @@
         def _():
             finish_user(1)
             for i in range(32):
-                for w in range(3):
-                    ids[w, i:i + 1, :] = tri[w:w + 1, i * 128:(i + 1) * 128] & ((4096 if w == 0 else QUART) - 1)
+                for w, ids in enumerate((id_u, id_p, id_n)):
+                    ids[i:i + 1, :] = tri[w:w + 1, i * 128:(i + 1) * 128] & ((4096 if w == 0 else 2 * QUART) - 1)
 
         @pl.when(t == 5)
         def _():
@@ -370,6 +386,9 @@
         @pl.when(t == D2)
         def _():
             cp_y(3).start()
+
+    cp_o(NCH - 1, r_par).wait_recv()
+    store(out_p, NCH - 1, r_par, p_sem).start()
 
     last = LAYERS * NCH
     for g in range(last - 2, last):
@@ -385,11 +404,17 @@
     def _(j):
         for rel, dev in ((0, par), (1, xpe), (2, xpa)):
             cs_copy(rel, j, dev).wait_send()
+        cp_o(j, r).wait_send()
+        store(out_i, j, r, l_sem).wait()
+        store(out_p, j, r_par, p_sem).wait()
 
     @pl.loop(0, 3 * NCH)
     def _(i):
-        ag_x(i // NCH, i % NCH, r).wait_send()
-        ag_d(i // NCH, i % NCH, r).wait_send()
+        @pl.when(i // NCH != 1)
+        def _():
+            ag_x(i // NCH, i % NCH, r).wait_send()
+            ag_d(i // NCH, i % NCH, r).wait_send()
+
         ag_f(i // NCH, i % NCH, r_xp).wait_send()
 
 
@@ -399,10 +424,10 @@
     vmem = pl.BlockSpec(memory_space=pltpu.VMEM)
     return pl.pallas_call(
         _main_kernel,
-        out_shape=(jax.ShapeDtypeStruct((EMB, QUART), BF), jax.ShapeDtypeStruct((8, EMB, HALF), BF),
-                   jax.ShapeDtypeStruct((3, 32, 128), jnp.int32)),
+        out_shape=(jax.ShapeDtypeStruct((EMB, QUART), BF), jax.ShapeDtypeStruct((EMB, QUART), BF),
+                   jax.ShapeDtypeStruct((8, EMB, HALF), BF), *[jax.ShapeDtypeStruct((32, 128), jnp.int32)] * 3),
         in_specs=[any_spec, any_spec, any_spec, vmem],
-        out_specs=(vmem, vmem, vmem),
+        out_specs=(any_spec, any_spec, vmem, vmem, vmem, vmem),
         scratch_shapes=[
             pltpu.VMEM((NBLK, USERS, CH), F8),
             pltpu.VMEM((RING, PIECE, CH), jnp.int32),
@@ -420,56 +445,61 @@
             dma((3 * NCH,)), dma((3 * NCH,)), dma((3 * NCH,)), dma((3 * NCH,)), dma((3 * NCH,)), dma((3 * NCH,)),
             dma((3, NCH)), dma((3, NCH)), dma((1,)), dma((1,)),
             dma((2,)), dma((2,)), dma((4,)), dma((4,)), dma((4,)), dma((8,)),
-            dma((3,)), dma((3,)), dma((3,)), dma((3,)), dma((7,)), dma((7,)),
+            dma((3,)), dma((3,)), dma((3,)), dma((3,)), dma((7,)), dma((7,)), dma((NCH,)), dma((NCH,)), dma((NCH,)), dma((NCH,)),
         ],
         compiler_params=pltpu.CompilerParams(collective_id=0, has_side_effects=True, vmem_limit_bytes=67043328),
         name="propagate",
     )(mask, eu0, ei0, tri)
 
 
-def _lookup_kernel(uid, pid, nid, tri, items, users, part, out_i, out_u, it, ut, pp, pn):
+def _lookup_kernel(uid, pid, nid, tri, items, items_p, users, part, out_i, out_u, it, ut, pp, pn):
     c = lax.axis_index("col")
     r = lax.axis_index("row")
+    k = r % 2
     out_i[...] = items[...]
     out_u[...] = users[2 * r + c]
-    for i in range(QUART // 512):
-        it[i * 512:(i + 1) * 512, :EMB] = items[:, i * 512:(i + 1) * 512].astype(F32).T
+    for src, at in ((items, k * QUART), (items_p, (1 - k) * QUART)):
+        for i in range(QUART // 512):
+            rows = pl.ds(pl.multiple_of(at + i * 512, 512), 512)
+            it[rows, :EMB] = src[:, i * 512:(i + 1) * 512].astype(F32).T
     for i in range(8):
         ut[i * HALF:(i + 1) * HALF, :EMB] = users[i].astype(F32).T
 
-    @pl.loop(0, 4096 // 64)
+    @pl.loop(0, 2048 // 64)
     def _(i):
         for w in range(64):
             t = i * 64 + w
-            u = ut[pl.ds(uid[t], 1), :]
-            pp[pl.ds(t, 1), :] = u * it[pl.ds(pid[t], 1), :]
-            pn[pl.ds(t, 1), :] = u * it[pl.ds(nid[t], 1), :]
-
-    @pl.loop(0, 8)
+            g = k * 2048 + t
+            u = ut[pl.ds(uid[g], 1), :]
+            pp[pl.ds(t, 1), :] = u * it[pl.ds(pid[g], 1), :]
+            pn[pl.ds(t, 1), :] = u * it[pl.ds(nid[g], 1), :]
+
+    @pl.loop(0, 4)
     def _(i):
         for w in range(4):
             at = i * 4 + w
             rows = pl.ds(pl.multiple_of(at * 128, 128), 128)
+            cols = pl.ds(pl.multiple_of(k * 2048 + at * 128, 128), 128)
             sp = jnp.sum(pp[rows, :].T[:EMB], axis=0, keepdims=True)
             sn = jnp.sum(pn[rows, :].T[:EMB], axis=0, keepdims=True)
-            own_p = tri[1:2, rows] // QUART == c * 4 + r
-            own_n = tri[2:3, rows] // QUART == c * 4 + r
+            own_p = tri[1:2, cols] // (2 * QUART) == 2 * c + r // 2
+            own_n = tri[2:3, cols] // (2 * QUART) == 2 * c + r // 2
             part[pl.ds(at, 1), :] = jnp.where(own_p, sp, 0.0) - jnp.where(own_n, sn, 0.0)
 
 
-def _lookup(ids, tri, items, users):
+def _lookup(ids, tri, items, items_p, users):
     vmem = pl.BlockSpec(memory_space=pltpu.VMEM)
     smem = pl.BlockSpec(memory_space=pltpu.SMEM)
     return pl.pallas_call(
         _lookup_kernel,
-        out_shape=(jax.ShapeDtypeStruct((32, 128), F32), jax.ShapeDtypeStruct((EMB, QUART), BF),
+        out_shape=(jax.ShapeDtypeStruct((16, 128), F32), jax.ShapeDtypeStruct((EMB, QUART), BF),
                    jax.ShapeDtypeStruct((EMB, HALF), BF)),
-        in_specs=[smem, smem, smem, vmem, vmem, vmem],
+        in_specs=[smem, smem, smem, vmem, vmem, vmem, vmem],
         out_specs=(vmem, vmem, vmem),
-        scratch_shapes=[pltpu.VMEM((QUART, 128), F32), pltpu.VMEM((4096, 128), F32),
-                        pltpu.VMEM((4096, 128), F32), pltpu.VMEM((4096, 128), F32)],
+        scratch_shapes=[pltpu.VMEM((2 * QUART, 128), F32), pltpu.VMEM((4096, 128), F32),
+                        pltpu.VMEM((2048, 128), F32), pltpu.VMEM((2048, 128), F32)],
         name="lookup",
-    )(ids[0].reshape(4096), ids[1].reshape(4096), ids[2].reshape(4096), tri, items, users)
+    )(*[i.reshape(4096) for i in ids], tri, items, items_p, users)
 
 
 def _loss_kernel(part, out, got, s_sem, r_sem):
@@ -496,10 +526,9 @@
     got[me] = part[...]
     for i in range(1, 8):
         copy(i, sender(i)).wait()
-    m = got[0]
-    for i in range(1, 8):
-        m = m + got[i]
-    out[...] = jnp.maximum(-m, 0.0) + jnp.log1p(jnp.exp(-jnp.abs(m)))
+    for h in range(2):
+        m = (got[2 * h] + got[2 * h + 1]) + (got[2 * h + 4] + got[2 * h + 5])
+        out[h * 16:(h + 1) * 16, :] = jnp.maximum(-m, 0.0) + jnp.log1p(jnp.exp(-jnp.abs(m)))
 
 
 def _loss(part):
@@ -509,7 +538,7 @@
         out_shape=jax.ShapeDtypeStruct((32, 128), F32),
         in_specs=[vmem],
         out_specs=vmem,
-        scratch_shapes=[pltpu.VMEM((8, 32, 128), F32), pltpu.SemaphoreType.DMA((8,)), pltpu.SemaphoreType.DMA((8,))],
+        scratch_shapes=[pltpu.VMEM((8, 16, 128), F32), pltpu.SemaphoreType.DMA((8,)), pltpu.SemaphoreType.DMA((8,))],
         compiler_params=pltpu.CompilerParams(collective_id=1, has_side_effects=True),
         name="loss",
     )(part)
@@ -518,8 +547,8 @@
 def solution(mesh):
     def device_body(mask_blk, user_shard, item_shard, triples):
         tri = triples.T
-        out_it, users, ids = _main(mask_blk, user_shard.T, item_shard.T, tri)
-        part, out_it, out_ut = _lookup(ids, tri, out_it, users)
+        out_it, par_it, users, *ids = _main(mask_blk, user_shard.T, item_shard.T, tri)
+        part, out_it, out_ut = _lookup(ids, tri, out_it, par_it, users)
         bpr_loss = _loss(part).reshape(4096)
         return out_ut.T, out_it.T, bpr_loss
 

time: 260 us -> 256 us (0.985)
    pallas_call x1, Pallas kernels: 12.8 us -> 9.31 us  [_lookup(): pl.pallas_call(_lookup_kernel, out_shape=(jax.ShapeDtypeStruct((16, 128),...]
where the time goes in v5:
time: 256 us
  Pallas kernels  254 us (99%)
    pallas_call x1, Pallas kernels, _main(): pl.pallas_call(_main_kernel, out_shape=(jax.ShapeDtypeStruct((EMB, QUART)...  238 us
    pallas_call x1, Pallas kernels, _lookup(): pl.pallas_call(_lookup_kernel, out_shape=(jax.ShapeDtypeStruct((16, 128),...  9.31 us
    pallas_call x1, Pallas kernels, _loss(): pl.pallas_call(_loss_kernel, out_shape=jax.ShapeDtypeStruct((32, 128), F3...  6.49 us

profile of v5, /device:TPU:0, one launch (start us, length us, event | category | flops | bytes accessed | tf_op | source)
XLA Modules:
  0.0 256.0 jit_solution(5492141662687446423)
XLA Ops:
  0.6 238.2 %propagate.1 = (bf16[64,8192]{1,0:T(8,128)(2,1)}, bf16[64,8192]{1,0:T(8,128)(2,1)}, bf16[8,64,512]{2,1,0:T(8,128)(2,1)}, s32[32,128]{1,0:T(8,128)}, s32[32,128]{1,0:T(8,128)}, /*index=5*/s32[32,128]{1,0:T(8,128)}) custom-call(s32[1024,32768]{1,0:T(8,128)} %mask.1, bf16[64,512]{1,0:T(8,128)(2,1)} %bitcast.12, bf16[64,8192]{1,0:T(8,128)(2,1)} %bitcast.9, ...), custom_call_target="tpu_custom_call" | custom-call | tf_op jit(solution)/shard_map/propagate/pallas_call | solution.py:425
  238.9 9.3 %lookup.1 = (f32[16,128]{1,0:T(8,128)}, bf16[64,8192]{1,0:T(8,128)(2,1)}, bf16[64,512]{1,0:T(8,128)(2,1)}) custom-call(s32[4096]{0:T(1024)} %bitcast.14, s32[4096]{0:T(1024)} %bitcast.15, s32[4096]{0:T(1024)} %bitcast.16, s32[3,4096]{1,0:T(4,128)} %bitcast.11, bf16[64,8192]{1,0:T(8,128)(2,1)} %get-tuple-element.15.items, ...), custom_call_target="tpu_custom_call" | custom-call | tf_op jit(solution)/shard_map/lookup/pallas_call | solution.py:493
  248.2 6.5 %loss.1 = f32[32,128]{1,0:T(8,128)} custom-call(f32[16,128]{1,0:T(8,128)} %get-tuple-element.20.part), custom_call_target="tpu_custom_call" | custom-call | tf_op jit(solution)/shard_map/loss/pallas_call | solution.py:536
  254.7 1.3 copy.8

commit v6 on v5

--- a/solution.py
+++ b/solution.py
@@ -32,11 +32,11 @@
     return (val.reshape(rows // 8, 8, cols) * s8[None]).reshape(rows, cols)
 
 
-def _main_kernel(mask, eu0, ei0, tri, out_i, out_p, ua, id_u, id_p, id_n,
+def _main_kernel(mask, eu0, ei0, tri_in, out_i, out_p, ua, id_u, id_p, id_n,
                  m8, stage, pan, snd_a, rcv_a, snd_b, rcv_b, xs, xr,
                  uacc, yr, raw, eus, cs, csr, sib, cacc, rs, rsum, rsum_r, su,
                  st_sem, ld_sem, agx_s, agx_r, agd_s, agd_r, agf_s, agf_r, cs_s, cs_r,
-                 rs_s, rs_r, a_s, a_r, b_s, b_r, x_s, x_r, y_s, y_r, w_s, w_r, g_s, g_r, o_s, o_r, l_sem, p_sem):
+                 rs_s, rs_r, a_s, a_r, b_s, b_r, x_s, x_r, y_s, y_r, w_s, w_r, g_s, g_r, o_s, o_r, l_sem, tri):
     c = lax.axis_index("col")
     r = lax.axis_index("row")
     x = r // 2
@@ -65,11 +65,13 @@
                                      pan.at[0, j * 4 + r], ld_sem.at[j])
 
     user_load = pltpu.make_async_copy(eu0, raw.at[0, c], ld_sem.at[NCH])
+    tri_load = pltpu.make_async_copy(tri_in, tri, ld_sem.at[NCH + 1])
     for j in range(NCH):
         own_load(j).start()
     user_load.start()
     for p in range(RING):
         piece(p).start()
+    tri_load.start()
 
     barrier = pltpu.get_barrier_semaphore()
     for cc in range(2):
@@ -227,11 +229,10 @@
         cp_b(g).start()
 
     def cp_o(j, q):
-        ref = pan.at[1, j * 4 + q]
-        return rcopy(ref, ref, o_s.at[j], o_r.at[j], par)
-
-    def store(out, j, q, sem):
-        return pltpu.make_async_copy(pan.at[1, j * 4 + q], out.at[:, pl.ds(pl.multiple_of(j * CH, CH), CH)], sem.at[j])
+        return rcopy(pan.at[1, j * 4 + q], out_p.at[:, pl.ds(pl.multiple_of(j * CH, CH), CH)], o_s.at[j], o_r.at[j], par)
+
+    def store(j):
+        return pltpu.make_async_copy(pan.at[1, j * 4 + r], out_i.at[:, pl.ds(pl.multiple_of(j * CH, CH), CH)], l_sem.at[j])
 
     def step_b(g):
         lay = g // NCH
@@ -256,12 +257,7 @@
             ag_d(1, j, r).wait_send()
             pan[1, b] = (tot * 0.25).astype(BF)
             cp_o(j, r).start()
-            store(out_i, j, r, l_sem).start()
-
-            @pl.when(j >= 1)
-            def _():
-                cp_o(j - 1, r_par).wait_recv()
-                store(out_p, j - 1, r_par, p_sem).start()
+            store(j).start()
 
     def step_c(g):
         a = g // NCH + 1
@@ -322,6 +318,7 @@
         @pl.when(t == 4)
         def _():
             finish_user(1)
+            tri_load.wait()
             for i in range(32):
                 for w, ids in enumerate((id_u, id_p, id_n)):
                     ids[i:i + 1, :] = tri[w:w + 1, i * 128:(i + 1) * 128] & ((4096 if w == 0 else 2 * QUART) - 1)
@@ -386,9 +383,6 @@
         @pl.when(t == D2)
         def _():
             cp_y(3).start()
-
-    cp_o(NCH - 1, r_par).wait_recv()
-    store(out_p, NCH - 1, r_par, p_sem).start()
 
     last = LAYERS * NCH
     for g in range(last - 2, last):
@@ -404,9 +398,8 @@
     def _(j):
         for rel, dev in ((0, par), (1, xpe), (2, xpa)):
             cs_copy(rel, j, dev).wait_send()
-        cp_o(j, r).wait_send()
-        store(out_i, j, r, l_sem).wait()
-        store(out_p, j, r_par, p_sem).wait()
+        cp_o(j, r).wait()
+        store(j).wait()
 
     @pl.loop(0, 3 * NCH)
     def _(i):
@@ -426,7 +419,7 @@
         _main_kernel,
         out_shape=(jax.ShapeDtypeStruct((EMB, QUART), BF), jax.ShapeDtypeStruct((EMB, QUART), BF),
                    jax.ShapeDtypeStruct((8, EMB, HALF), BF), *[jax.ShapeDtypeStruct((32, 128), jnp.int32)] * 3),
-        in_specs=[any_spec, any_spec, any_spec, vmem],
+        in_specs=[any_spec, any_spec, any_spec, any_spec],
         out_specs=(any_spec, any_spec, vmem, vmem, vmem, vmem),
         scratch_shapes=[
             pltpu.VMEM((NBLK, USERS, CH), F8),
@@ -441,29 +434,38 @@
             pltpu.VMEM((NBLK, 8, CH), F32), pltpu.VMEM((8, CH), F32),
             pltpu.VMEM((USERS, 128), F32), pltpu.VMEM((8, USERS), F32), pltpu.VMEM((8, USERS), F32),
             pltpu.VMEM((2, 8, HALF), F32),
-            dma((RING,)), dma((NCH + 1,)),
+            dma((RING,)), dma((NCH + 2,)),
             dma((3 * NCH,)), dma((3 * NCH,)), dma((3 * NCH,)), dma((3 * NCH,)), dma((3 * NCH,)), dma((3 * NCH,)),
             dma((3, NCH)), dma((3, NCH)), dma((1,)), dma((1,)),
             dma((2,)), dma((2,)), dma((4,)), dma((4,)), dma((4,)), dma((8,)),
-            dma((3,)), dma((3,)), dma((3,)), dma((3,)), dma((7,)), dma((7,)), dma((NCH,)), dma((NCH,)), dma((NCH,)), dma((NCH,)),
+            dma((3,)), dma((3,)), dma((3,)), dma((3,)), dma((7,)), dma((7,)), dma((NCH,)), dma((NCH,)), dma((NCH,)), pltpu.VMEM((3, 4096), jnp.int32),
         ],
         compiler_params=pltpu.CompilerParams(collective_id=0, has_side_effects=True, vmem_limit_bytes=67043328),
         name="propagate",
     )(mask, eu0, ei0, tri)
 
 
-def _lookup_kernel(uid, pid, nid, tri, items, items_p, users, part, out_i, out_u, it, ut, pp, pn):
+def _lookup_kernel(uid, pid, nid, tri, items, items_p, users_in, part, out_i, out_u, it, ut, pp, pn, vi, users, sem):
     c = lax.axis_index("col")
     r = lax.axis_index("row")
     k = r % 2
-    out_i[...] = items[...]
-    out_u[...] = users[2 * r + c]
-    for src, at in ((items, k * QUART), (items_p, (1 - k) * QUART)):
+    loads = [pltpu.make_async_copy(users_in, users, sem.at[0]), pltpu.make_async_copy(items, vi.at[0], sem.at[1]),
+             pltpu.make_async_copy(items_p, vi.at[1], sem.at[2])]
+    for load in loads:
+        load.start()
+    put_u = pltpu.make_async_copy(users.at[2 * r + c], out_u, sem.at[3])
+    put_i = pltpu.make_async_copy(vi.at[0], out_i, sem.at[4])
+    loads[0].wait()
+    put_u.start()
+    for i in range(8):
+        ut[i * HALF:(i + 1) * HALF, :EMB] = users[i].astype(F32).T
+    for n, at in ((0, k * QUART), (1, (1 - k) * QUART)):
+        loads[1 + n].wait()
+        if n == 0:
+            put_i.start()
         for i in range(QUART // 512):
             rows = pl.ds(pl.multiple_of(at + i * 512, 512), 512)
-            it[rows, :EMB] = src[:, i * 512:(i + 1) * 512].astype(F32).T
-    for i in range(8):
-        ut[i * HALF:(i + 1) * HALF, :EMB] = users[i].astype(F32).T
+            it[rows, :EMB] = vi[n, :, i * 512:(i + 1) * 512].astype(F32).T
 
     @pl.loop(0, 2048 // 64)
     def _(i):
@@ -486,18 +488,23 @@
             own_n = tri[2:3, cols] // (2 * QUART) == 2 * c + r // 2
             part[pl.ds(at, 1), :] = jnp.where(own_p, sp, 0.0) - jnp.where(own_n, sn, 0.0)
 
+    put_u.wait()
+    put_i.wait()
+
 
 def _lookup(ids, tri, items, items_p, users):
     vmem = pl.BlockSpec(memory_space=pltpu.VMEM)
     smem = pl.BlockSpec(memory_space=pltpu.SMEM)
+    any_spec = pl.BlockSpec(memory_space=pl.ANY)
     return pl.pallas_call(
         _lookup_kernel,
         out_shape=(jax.ShapeDtypeStruct((16, 128), F32), jax.ShapeDtypeStruct((EMB, QUART), BF),
                    jax.ShapeDtypeStruct((EMB, HALF), BF)),
-        in_specs=[smem, smem, smem, vmem, vmem, vmem, vmem],
-        out_specs=(vmem, vmem, vmem),
+        in_specs=[smem, smem, smem, vmem, any_spec, any_spec, any_spec],
+        out_specs=(vmem, any_spec, any_spec),
         scratch_shapes=[pltpu.VMEM((2 * QUART, 128), F32), pltpu.VMEM((4096, 128), F32),
-                        pltpu.VMEM((2048, 128), F32), pltpu.VMEM((2048, 128), F32)],
+                        pltpu.VMEM((2048, 128), F32), pltpu.VMEM((2048, 128), F32),
+                        pltpu.VMEM((2, EMB, QUART), BF), pltpu.VMEM((8, EMB, HALF), BF), pltpu.SemaphoreType.DMA((5,))],
         name="lookup",
     )(*[i.reshape(4096) for i in ids], tri, items, items_p, users)
 

time: 256 us -> 255 us (level)
  no operation moved by 1% of the time
where the time goes in v6:
time: 255 us
  Pallas kernels  253 us (99%)
    pallas_call x1, Pallas kernels, _main(): pl.pallas_call(_main_kernel, out_shape=(jax.ShapeDtypeStruct((EMB, QUART)...  237 us
    pallas_call x1, Pallas kernels, _lookup(): pl.pallas_call(_lookup_kernel, out_shape=(jax.ShapeDtypeStruct((16, 128),...  9.98 us
    pallas_call x1, Pallas kernels, _loss(): pl.pallas_call(_loss_kernel, out_shape=jax.ShapeDtypeStruct((32, 128), F3...  6.11 us

profile of v6, /device:TPU:0, one launch (start us, length us, event | category | flops | bytes accessed | tf_op | source)
XLA Modules:
  0.0 254.9 jit_solution(7477213269970306964)
XLA Ops:
  0.6 236.8 %propagate.1 = (bf16[64,8192]{1,0:T(8,128)(2,1)}, bf16[64,8192]{1,0:T(8,128)(2,1)}, bf16[8,64,512]{2,1,0:T(8,128)(2,1)}, s32[32,128]{1,0:T(8,128)}, s32[32,128]{1,0:T(8,128)}, /*index=5*/s32[32,128]{1,0:T(8,128)}) custom-call(s32[1024,32768]{1,0:T(8,128)} %mask.1, bf16[64,512]{1,0:T(8,128)(2,1)} %bitcast.12, bf16[64,8192]{1,0:T(8,128)(2,1)} %bitcast.9, ...), custom_call_target="tpu_custom_call" | custom-call | tf_op jit(solution)/shard_map/propagate/pallas_call | solution.py:418
  237.5 10.0 %lookup.1 = (f32[16,128]{1,0:T(8,128)}, bf16[64,8192]{1,0:T(8,128)(2,1)}, bf16[64,512]{1,0:T(8,128)(2,1)}) custom-call(s32[4096]{0:T(1024)} %bitcast.14, s32[4096]{0:T(1024)} %bitcast.15, s32[4096]{0:T(1024)} %bitcast.16, s32[3,4096]{1,0:T(4,128)} %bitcast.11, bf16[64,8192]{1,0:T(8,128)(2,1)} %get-tuple-element.15.items, ...), custom_call_target="tpu_custom_call" | custom-call | tf_op jit(solution)/shard_map/lookup/pallas_call | solution.py:499
  247.4 6.1 %loss.1 = f32[32,128]{1,0:T(8,128)} custom-call(f32[16,128]{1,0:T(8,128)} %get-tuple-element.20.part), custom_call_target="tpu_custom_call" | custom-call | tf_op jit(solution)/shard_map/loss/pallas_call | solution.py:543
  253.6 1.3 copy.8

commit v7 on v6

--- a/solution.py
+++ b/solution.py
@@ -20,7 +20,7 @@
 NBLK = 32
 PIECE = 256
 STEP = 64
-RING = 7
+RING = 8
 UP_U, DN_U = 256.0, 1.0 / 256.0
 UP_I, DN_I = 64.0, 1.0 / 64.0
 LAG_B, LAG_C, LAG_D = 2, 3, 4
@@ -161,21 +161,26 @@
 
             cs[b] = jnp.sum(cacc[...], axis=0, keepdims=True)
 
-        for rel, dev in ((0, par), (1, xpe), (2, xpa)):
-            cs_copy(rel, g, dev).start()
-
-        @pl.when(g + AHEAD < NCH)
-        def _():
-            ag_x(0, g + AHEAD, r).start()
-
         @pl.when(g == NCH - 1)
         def _():
             rsum[...] = lax.dot_general(jnp.ones((8, 128), BF), rs[...].astype(BF), (((1,), (1,)), ((), ())),
                                         preferred_element_type=F32)
             cp_deg.start()
 
-        ag_x(0, g, r_xp).wait_recv()
-        ag_f(0, g, r_xp).start()
+        for rel, dev in ((0, par), (1, xpe), (2, xpa)):
+            cs_copy(rel, g, dev).start()
+
+        @pl.when(g + AHEAD < NCH)
+        def _():
+            ag_x(0, g + AHEAD, r).start()
+
+        @pl.when(g >= 1)
+        def _():
+            ag_x(0, g - 1, r_xp).wait_recv()
+            ag_f(0, g - 1, r_xp).start()
+
+    ag_x(0, NCH - 1, r_xp).wait_recv()
+    ag_f(0, NCH - 1, r_xp).start()
 
     cp_deg.wait()
     w0.wait()
@@ -445,27 +450,18 @@
     )(mask, eu0, ei0, tri)
 
 
-def _lookup_kernel(uid, pid, nid, tri, items, items_p, users_in, part, out_i, out_u, it, ut, pp, pn, vi, users, sem):
+def _lookup_kernel(uid, pid, nid, tri, items, items_p, users, part, out_i, out_u, it, ut, pp, pn):
     c = lax.axis_index("col")
     r = lax.axis_index("row")
     k = r % 2
-    loads = [pltpu.make_async_copy(users_in, users, sem.at[0]), pltpu.make_async_copy(items, vi.at[0], sem.at[1]),
-             pltpu.make_async_copy(items_p, vi.at[1], sem.at[2])]
-    for load in loads:
-        load.start()
-    put_u = pltpu.make_async_copy(users.at[2 * r + c], out_u, sem.at[3])
-    put_i = pltpu.make_async_copy(vi.at[0], out_i, sem.at[4])
-    loads[0].wait()
-    put_u.start()
+    out_i[...] = items[...]
+    out_u[...] = users[2 * r + c]
+    for src, at in ((items, k * QUART), (items_p, (1 - k) * QUART)):
+        for i in range(QUART // 512):
+            rows = pl.ds(pl.multiple_of(at + i * 512, 512), 512)
+            it[rows, :EMB] = src[:, i * 512:(i + 1) * 512].astype(F32).T
     for i in range(8):
         ut[i * HALF:(i + 1) * HALF, :EMB] = users[i].astype(F32).T
-    for n, at in ((0, k * QUART), (1, (1 - k) * QUART)):
-        loads[1 + n].wait()
-        if n == 0:
-            put_i.start()
-        for i in range(QUART // 512):
-            rows = pl.ds(pl.multiple_of(at + i * 512, 512), 512)
-            it[rows, :EMB] = vi[n, :, i * 512:(i + 1) * 512].astype(F32).T
 
     @pl.loop(0, 2048 // 64)
     def _(i):
@@ -488,36 +484,34 @@
             own_n = tri[2:3, cols] // (2 * QUART) == 2 * c + r // 2
             part[pl.ds(at, 1), :] = jnp.where(own_p, sp, 0.0) - jnp.where(own_n, sn, 0.0)
 
-    put_u.wait()
-    put_i.wait()
-
 
 def _lookup(ids, tri, items, items_p, users):
     vmem = pl.BlockSpec(memory_space=pltpu.VMEM)
     smem = pl.BlockSpec(memory_space=pltpu.SMEM)
-    any_spec = pl.BlockSpec(memory_space=pl.ANY)
     return pl.pallas_call(
         _lookup_kernel,
         out_shape=(jax.ShapeDtypeStruct((16, 128), F32), jax.ShapeDtypeStruct((EMB, QUART), BF),
                    jax.ShapeDtypeStruct((EMB, HALF), BF)),
-        in_specs=[smem, smem, smem, vmem, any_spec, any_spec, any_spec],
-        out_specs=(vmem, any_spec, any_spec),
+        in_specs=[smem, smem, smem, vmem, vmem, vmem, vmem],
+        out_specs=(vmem, vmem, vmem),
         scratch_shapes=[pltpu.VMEM((2 * QUART, 128), F32), pltpu.VMEM((4096, 128), F32),
-                        pltpu.VMEM((2048, 128), F32), pltpu.VMEM((2048, 128), F32),
-                        pltpu.VMEM((2, EMB, QUART), BF), pltpu.VMEM((8, EMB, HALF), BF), pltpu.SemaphoreType.DMA((5,))],
+                        pltpu.VMEM((2048, 128), F32), pltpu.VMEM((2048, 128), F32)],
         name="lookup",
     )(*[i.reshape(4096) for i in ids], tri, items, items_p, users)
 
 
-def _loss_kernel(part, out, got, s_sem, r_sem):
+def _loss_kernel(part_in, out, got, part, s_sem, r_sem):
     c = lax.axis_index("col")
     r = lax.axis_index("row")
     me = 2 * r + c
+    load = pltpu.make_async_copy(part_in, part, s_sem.at[0])
+    load.start()
     barrier = pltpu.get_barrier_semaphore()
     for cc in range(2):
         for rr in range(4):
             pl.semaphore_signal(barrier, inc=1, device_id=(cc, rr), device_id_type=MESH)
     pl.semaphore_wait(barrier, 8)
+    load.wait()
 
     def copy(i, slot):
         dr, dc = i // 2, i % 2
@@ -543,9 +537,9 @@
     return pl.pallas_call(
         _loss_kernel,
         out_shape=jax.ShapeDtypeStruct((32, 128), F32),
-        in_specs=[vmem],
+        in_specs=[pl.BlockSpec(memory_space=pl.ANY)],
         out_specs=vmem,
-        scratch_shapes=[pltpu.VMEM((8, 16, 128), F32), pltpu.SemaphoreType.DMA((8,)), pltpu.SemaphoreType.DMA((8,))],
+        scratch_shapes=[pltpu.VMEM((8, 16, 128), F32), pltpu.VMEM((16, 128), F32), pltpu.SemaphoreType.DMA((8,)), pltpu.SemaphoreType.DMA((8,))],
         compiler_params=pltpu.CompilerParams(collective_id=1, has_side_effects=True),
         name="loss",
     )(part)

time: 255 us -> 254 us (level)
  no operation moved by 1% of the time
where the time goes in v7:
time: 254 us; the launch traced here: 253 us
  Pallas kernels  251 us (99%)
    pallas_call x1, Pallas kernels, _main(): pl.pallas_call(_main_kernel, out_shape=(jax.ShapeDtypeStruct((EMB, QUART)...  237 us
    pallas_call x1, Pallas kernels, _lookup(): pl.pallas_call(_lookup_kernel, out_shape=(jax.ShapeDtypeStruct((16, 128),...  9.31 us
    pallas_call x1, Pallas kernels, _loss(): pl.pallas_call(_loss_kernel, out_shape=jax.ShapeDtypeStruct((32, 128), F3...  5.41 us

profile of v7, /device:TPU:0, one launch (start us, length us, event | category | flops | bytes accessed | tf_op | source)
XLA Modules:
  0.0 253.3 jit_solution(16192258198947237326)
XLA Ops:
  0.6 236.6 %propagate.1 = (bf16[64,8192]{1,0:T(8,128)(2,1)}, bf16[64,8192]{1,0:T(8,128)(2,1)}, bf16[8,64,512]{2,1,0:T(8,128)(2,1)}, s32[32,128]{1,0:T(8,128)}, s32[32,128]{1,0:T(8,128)}, /*index=5*/s32[32,128]{1,0:T(8,128)}) custom-call(s32[1024,32768]{1,0:T(8,128)} %mask.1, bf16[64,512]{1,0:T(8,128)(2,1)} %bitcast.12, bf16[64,8192]{1,0:T(8,128)(2,1)} %bitcast.9, ...), custom_call_target="tpu_custom_call" | custom-call | tf_op jit(solution)/shard_map/propagate/pallas_call | solution.py:423
  237.3 9.3 %lookup.1 = (f32[16,128]{1,0:T(8,128)}, bf16[64,8192]{1,0:T(8,128)(2,1)}, bf16[64,512]{1,0:T(8,128)(2,1)}) custom-call(s32[4096]{0:T(1024)} %bitcast.14, s32[4096]{0:T(1024)} %bitcast.15, s32[4096]{0:T(1024)} %bitcast.16, s32[3,4096]{1,0:T(4,128)} %bitcast.11, bf16[64,8192]{1,0:T(8,128)(2,1)} %get-tuple-element.15.items, ...), custom_call_target="tpu_custom_call" | custom-call | tf_op jit(solution)/shard_map/lookup/pallas_call | solution.py:491
  246.6 5.4 %loss.1 = f32[32,128]{1,0:T(8,128)} custom-call(f32[16,128]{1,0:T(8,128)} %get-tuple-element.20.part_in), custom_call_target="tpu_custom_call" | custom-call | tf_op jit(solution)/shard_map/loss/pallas_call | solution.py:537
  252.0 1.3 copy.8

commit v8 on v7

--- a/solution.py
+++ b/solution.py
@@ -77,7 +77,6 @@
     for cc in range(2):
         for rr in range(4):
             pl.semaphore_signal(barrier, inc=1, device_id=(cc, rr), device_id_type=MESH)
-    pl.semaphore_wait(barrier, 8)
 
     def ag_x(a, j, q):
         i = a * NCH + j
@@ -93,15 +92,6 @@
         i = a * NCH + j
         ref = pan.at[a, j * 4 + q]
         return rcopy(ref, ref, agf_s.at[i], agf_r.at[i], par)
-
-    for j in range(NCH):
-        own_load(j).wait()
-        if j < AHEAD:
-            ag_x(0, j, r).start()
-        ag_d(0, j, r).start()
-    user_load.wait()
-    w0 = rcopy(raw.at[0, c], raw.at[0, c], w_s.at[0], w_r.at[0], ype)
-    w0.start()
 
     rs[...] = jnp.zeros_like(rs)
     uacc[...] = jnp.zeros_like(uacc)
@@ -130,8 +120,7 @@
 
     cp_deg = rcopy(rsum, rsum_r, rs_s.at[0], rs_r.at[0], ype)
 
-    @pl.loop(0, NCH)
-    def _(g):
+    def take_group(g):
         @pl.loop(0, 4)
         def _(q):
             b = g * 4 + q
@@ -161,6 +150,25 @@
 
             cs[b] = jnp.sum(cacc[...], axis=0, keepdims=True)
 
+    take_group(0)
+    pl.semaphore_wait(barrier, 8)
+    for j in range(NCH):
+        own_load(j).wait()
+        if j < AHEAD:
+            ag_x(0, j, r).start()
+        ag_d(0, j, r).start()
+    user_load.wait()
+    w0 = rcopy(raw.at[0, c], raw.at[0, c], w_s.at[0], w_r.at[0], ype)
+    w0.start()
+
+    for rel, dev in ((0, par), (1, xpe), (2, xpa)):
+        cs_copy(rel, 0, dev).start()
+    ag_x(0, AHEAD, r).start()
+
+    @pl.loop(1, NCH)
+    def _(g):
+        take_group(g)
+
         @pl.when(g == NCH - 1)
         def _():
             rsum[...] = lax.dot_general(jnp.ones((8, 128), BF), rs[...].astype(BF), (((1,), (1,)), ((), ())),
@@ -174,10 +182,8 @@
         def _():
             ag_x(0, g + AHEAD, r).start()
 
-        @pl.when(g >= 1)
-        def _():
-            ag_x(0, g - 1, r_xp).wait_recv()
-            ag_f(0, g - 1, r_xp).start()
+        ag_x(0, g - 1, r_xp).wait_recv()
+        ag_f(0, g - 1, r_xp).start()
 
     ag_x(0, NCH - 1, r_xp).wait_recv()
     ag_f(0, NCH - 1, r_xp).start()

time: 254 us -> 253 us (level)
  no operation moved by 1% of the time
where the time goes in v8:
time: 253 us; the launch traced here: 252 us
  Pallas kernels  251 us (99%)
    pallas_call x1, Pallas kernels, _main(): pl.pallas_call(_main_kernel, out_shape=(jax.ShapeDtypeStruct((EMB, QUART)...  236 us
    pallas_call x1, Pallas kernels, _lookup(): pl.pallas_call(_lookup_kernel, out_shape=(jax.ShapeDtypeStruct((16, 128),...  9.31 us
    pallas_call x1, Pallas kernels, _loss(): pl.pallas_call(_loss_kernel, out_shape=jax.ShapeDtypeStruct((32, 128), F3...  5.41 us

profile of v8, /device:TPU:0, one launch (start us, length us, event | category | flops | bytes accessed | tf_op | source)
XLA Modules:
  0.0 252.5 jit_solution(10210088804873425409)
XLA Ops:
  0.6 235.8 %propagate.1 = (bf16[64,8192]{1,0:T(8,128)(2,1)}, bf16[64,8192]{1,0:T(8,128)(2,1)}, bf16[8,64,512]{2,1,0:T(8,128)(2,1)}, s32[32,128]{1,0:T(8,128)}, s32[32,128]{1,0:T(8,128)}, /*index=5*/s32[32,128]{1,0:T(8,128)}) custom-call(s32[1024,32768]{1,0:T(8,128)} %mask.1, bf16[64,512]{1,0:T(8,128)(2,1)} %bitcast.12, bf16[64,8192]{1,0:T(8,128)(2,1)} %bitcast.9, ...), custom_call_target="tpu_custom_call" | custom-call | tf_op jit(solution)/shard_map/propagate/pallas_call | solution.py:429
  236.4 9.3 %lookup.1 = (f32[16,128]{1,0:T(8,128)}, bf16[64,8192]{1,0:T(8,128)(2,1)}, bf16[64,512]{1,0:T(8,128)(2,1)}) custom-call(s32[4096]{0:T(1024)} %bitcast.14, s32[4096]{0:T(1024)} %bitcast.15, s32[4096]{0:T(1024)} %bitcast.16, s32[3,4096]{1,0:T(4,128)} %bitcast.11, bf16[64,8192]{1,0:T(8,128)(2,1)} %get-tuple-element.15.items, ...), custom_call_target="tpu_custom_call" | custom-call | tf_op jit(solution)/shard_map/lookup/pallas_call | solution.py:497
  245.7 5.4 %loss.1 = f32[32,128]{1,0:T(8,128)} custom-call(f32[16,128]{1,0:T(8,128)} %get-tuple-element.20.part_in), custom_call_target="tpu_custom_call" | custom-call | tf_op jit(solution)/shard_map/loss/pallas_call | solution.py:543
  251.2 1.3 copy.8
